TPU v7x, 32 devices: a whole 2x2x4 slice. The times are simulated.
32 devices in a mesh: gx: 8 (over z, x), gy: 4 (over y, core).
Axes of the slice: x: 2, y: 2, z: 4, core: 2. Of those that a mesh axis runs over, the one named last changes fastest.
Arguments:
- measures: bfloat16 [262144, 128], P(('gx', 'gy')), may hold values from -6 to 6
- row_keys: int32 [262144], P(('gx', 'gy')), may hold values from 0 to 16383, as said below
- orders: bfloat16 [16384, 128], P(('gx', 'gy')), may hold values from -6 to 6
- heavy_keys: int32 [64], replicated, may hold values from 0 to 16383, as said below
- key_slot: int32 [16384], replicated, may hold values from 0 to 16383, as said below
Outputs:
- result: bfloat16 [16384, 128], P(('gx', 'gy'))
- heavy_report: bfloat16 [64, 128], P(('gx', 'gy'))
- slot_rows: float32 [16384], P(('gx', 'gy'))
Inputs may be any that keep to these rules, and one draw needn't show every extreme that they name: `heavy_keys`: for each range block d, entries d * 2 to (d + 1) * 2 - 1 are distinct keys of d * 512 to (d + 1) * 512 - 1. `key_slot`: A permutation. Slot s belongs to owner s // 2048 and to quarter (s // 512) % q with q = 4. Key k lies in range block d = k // 512; every range block has exactly 64 keys with slots of each owner, all in quarter d % q. `row_keys`: in the rows of one device, among rows whose key is not heavy, at most 768 have slots of any one owner and at most 192 distinct keys have slots of any one owner; in every device both bounds are reached by some owner.
All inputs are finite; a program needn't handle non-finite values.
Results may differ from a plain program's by a relative error of at most 0.0021.
Values may be sent and summed in bfloat16 or wider, within the bound.
A program may use at most 64 MiB of HBM per device.

v0:
```python
import functools

import jax
import jax.numpy as jnp
from jax import lax
from jax.experimental import pallas as pl
from jax.experimental.pallas import tpu as pltpu
from jax.sharding import PartitionSpec as P

MESH = pl.DeviceIdType.MESH
LANES = 128
F32 = jnp.float32
BF16 = jnp.bfloat16
VMEM = pl.BlockSpec(memory_space=pltpu.VMEM)
ANY = pl.BlockSpec(memory_space=pl.ANY)
SMEM = pl.BlockSpec(memory_space=pltpu.SMEM)
LIMIT = 60 * 1024 * 1024
NN = (((1,), (0,)), ((), ()))
NT = (((1,), (1,)), ((), ()))


def dot(a, b, dims=NN):
    return lax.dot_general(a, b, dims, preferred_element_type=F32)


def iota(shape, dim):
    return lax.broadcasted_iota(jnp.int32, shape, dim)


def onehot(mask):
    return jnp.where(mask, 1.0, 0.0).astype(BF16)


def group_rank(flags, group_rows):
    rows = flags.shape[0]
    lane_r, lane_c = iota((LANES, LANES), 0), iota((LANES, LANES), 1)
    inside = dot(flags, onehot(lane_r < lane_c))
    whole = dot(flags, onehot(lane_r >= 0))
    row_r, row_c = iota((rows, rows), 0), iota((rows, rows), 1)
    earlier = onehot((row_c < row_r) & (row_r // group_rows == row_c // group_rows))
    return inside + dot(earlier, whole.astype(BF16))


def split(values):
    high = values.astype(BF16)
    low = (values - high.astype(F32)).astype(BF16)
    return jnp.concatenate([high, low], axis=1)


def eye(rows):
    return iota((rows, LANES), 0) == iota((rows, LANES), 1)


def encode(values):
    largest = jnp.max(jnp.abs(values), axis=1, keepdims=True)
    safe = jnp.maximum(largest, 1e-30)
    fixed = jnp.round(values * (1.0 / safe) * 32767.0).astype(jnp.int32).astype(jnp.int16)
    return fixed, jnp.sum(jnp.where(eye(values.shape[0]), safe, 0.0), axis=0, keepdims=True)


def decode(fixed, scale):
    column = jnp.sum(jnp.where(eye(fixed.shape[0]), scale, 0.0), axis=1, keepdims=True)
    return fixed.astype(jnp.int32).astype(F32) * (column * (1.0 / 32767.0))


def pieces(total):
    return [(at, min(LANES, total - at)) for at in range(0, total, LANES)]


def byte_table(table, parts):
    pieces = [((table >> (8 * p)) & 255).astype(F32).T for p in range(parts)]
    return jnp.concatenate(pieces, axis=0).astype(BF16)


def look_up(bytes_table, row_hot, column_mask, parts):
    wide = dot(bytes_table, row_hot)
    found = 0.0
    for p in range(parts):
        piece = wide[p * LANES : (p + 1) * LANES]
        found = found + float(256**p) * jnp.sum(
            jnp.where(column_mask, piece, 0.0), axis=0, keepdims=True
        )
    return found.astype(jnp.int32)


def byte_count(largest):
    return (int(largest).bit_length() + 7) // 8


def gather_rows(cfg, measures, keys, heavy, key_slot, send, tally, small, slots, sums):
    rows, block, nr = cfg["rows"], cfg["block"], cfg["nr"]
    segments, capacity = cfg["segments"], cfg["capacity"]
    slot_parts = byte_count(nr * LANES - 1)
    slot_bytes = byte_table(key_slot[...], slot_parts)
    hist_key = jnp.zeros((nr, LANES), F32)
    hist_slot = jnp.zeros((nr, LANES), F32)
    heavy_sum = jnp.zeros((cfg["heavy"], LANES), F32)
    for c in range(rows // block):
        span = slice(c * block, (c + 1) * block)
        key = keys[:, span]
        row_hot = onehot(iota((nr, block), 0) == key >> 7)
        column_mask = iota((LANES, block), 0) == (key & 127)
        hist_key = hist_key + dot(row_hot, onehot(column_mask), NT)
        heavy_hot = jnp.where(heavy[...] == key, 1.0, 0.0)
        is_heavy = jnp.max(heavy_hot, axis=0, keepdims=True) > 0.0
        heavy_sum = heavy_sum + dot(heavy_hot.astype(BF16), measures[span, :])
        slot = jnp.where(is_heavy, -1, look_up(slot_bytes, row_hot, column_mask, slot_parts))
        slots[:, span] = slot
        slot_row = onehot(iota((nr, block), 0) == slot >> 7)
        slot_column = onehot(iota((LANES, block), 0) == (slot & 127))
        hist_slot = hist_slot + dot(slot_row, slot_column, NT)
    present = hist_slot > 0.0
    group = cfg["own"] // LANES
    tally[...] = jnp.zeros(tally.shape, F32)
    for x in range(cfg["gx"]):
        tally[x, 0:group, :] = hist_slot[x * group : (x + 1) * group]
    rank = group_rank(onehot(present), group).astype(jnp.int32)
    owner = iota((nr, LANES), 0) // group
    segment_table = jnp.where(present, owner * capacity + rank + 1, 0)
    seg_parts = byte_count(segments)
    segment_bytes = byte_table(segment_table, seg_parts)
    step = cfg["seg_block"]
    for c in range(rows // block):
        span = slice(c * block, (c + 1) * block)
        slot = slots[:, span]
        slot_row = onehot(iota((nr, block), 0) == slot >> 7)
        slot_mask = iota((LANES, block), 0) == (slot & 127)
        segment = look_up(segment_bytes, slot_row, slot_mask, seg_parts) - 1
        for s in range(segments // step):
            hot = onehot(iota((step, block), 0) == segment - s * step)
            product = dot(hot, measures[span, :])
            place = slice(s * step, (s + 1) * step)
            if c == 0:
                sums[place, :] = product
            else:
                sums[place, :] += product
    for x in range(cfg["gx"]):
        for p, (at, size) in enumerate(pieces(capacity)):
            first = x * capacity + at
            fixed, scale = encode(sums[first : first + size, :])
            send[x, at : at + size, :] = fixed
            tally[x, group + p : group + p + 1, :] = scale
    each, key_rows, height = cfg["heavy_each"], cfg["key_rows"], cfg["height"]
    small[...] = jnp.zeros(small.shape, F32)
    for d in range(cfg["devices"]):
        small[d * height : d * height + each, :] = heavy_sum[d * each : (d + 1) * each]
        top = (d + 1) * height
        small[top - key_rows : top, :] = hist_key[d * key_rows : (d + 1) * key_rows]


def place_rows(cfg, got, got_tally, key_slot, send, scales, tally, spread, ranks):
    gx, gy, own, kpp = cfg["gx"], cfg["gy"], cfg["own"], cfg["kpp"]
    key_rows, capacity = cfg["key_rows"], cfg["capacity"]
    group = own // LANES
    base = lax.axis_index("gx") * own
    local = key_slot[...] - base
    mine = (local >= 0) & (local < own)
    rank = jnp.where(mine, group_rank(onehot(mine), key_rows), -1.0).astype(jnp.int32)
    local = local.astype(F32)
    for y in range(gy):
        for x in range(gx):
            first = (x * gy + y) * key_rows
            acc = jnp.zeros((kpp, LANES), F32)
            for j in range(key_rows):
                hit = iota((kpp, LANES), 0) == rank[first + j : first + j + 1]
                acc = acc + jnp.where(hit, local[first + j : first + j + 1], 0.0)
            at = (y * gx + x) * kpp
            spread[at : at + kpp, :] = acc
    counts = jnp.concatenate([got_tally[i, 0:group, :] for i in range(gx)], axis=0)
    present = counts > 0.0
    ranks[...] = jnp.where(present, group_rank(onehot(present), group) + 1.0, 0.0)
    total = counts[0:group]
    for i in range(1, gx):
        total = total + counts[i * group : (i + 1) * group]
    tally[...] = total
    values = []
    for i in range(gx):
        decoded = [
            decode(got[i, at : at + size, :], got_tally[i, group + p : group + p + 1, :])
            for p, (at, size) in enumerate(pieces(capacity))
        ]
        values.append(split(jnp.concatenate(decoded, axis=0)))
    quarter = own // gy
    for q in range(gy):
        at = slice(q * quarter, (q + 1) * quarter)
        slot = jnp.sum(spread[at, :], axis=1, keepdims=True).astype(jnp.int32) - q * quarter
        found = jnp.zeros((quarter, gx), F32)
        for j in range(key_rows):
            hot = onehot(slot - j * LANES == iota((quarter, LANES), 1))
            table = ranks[pl.ds(q * key_rows + j, gx, stride=group), :].astype(BF16)
            found = found + dot(hot, table, NT)
        found = found.astype(jnp.int32) - 1
        out = jnp.zeros((quarter, 2 * LANES), F32)
        for i in range(gx):
            hot = onehot(found[:, i : i + 1] == iota((quarter, capacity), 1))
            out = out + dot(hot, values[i])
        out = out[:, :LANES] + out[:, LANES:]
        for x in range(gx):
            fixed, scale = encode(out[x * kpp : (x + 1) * kpp])
            send[q * gx + x] = fixed
            scales[q * gx + x] = scale


def join_rows(cfg, heavy, got, got_scales, got_small, got_tally, orders, key_slot, result, report, slot_rows, sums, joined):
    gx, gy, own, kpp = cfg["gx"], cfg["gy"], cfg["own"], cfg["kpp"]
    key_rows, height, each = cfg["key_rows"], cfg["height"], cfg["heavy_each"]
    key_dev = key_rows * LANES
    device = lax.axis_index("gx") * gy + lax.axis_index("gy")
    total = got_tally[0:key_rows]
    for y in range(1, gy):
        total = total + got_tally[y * key_rows : (y + 1) * key_rows]
    slot_rows[...] = total
    small = got_small[0:height]
    for d in range(1, cfg["devices"]):
        small = small + got_small[d * height : (d + 1) * height]
    for x in range(gx):
        part = decode(got[x * gy], got_scales[x * gy])
        for y in range(1, gy):
            part = part + decode(got[x * gy + y], got_scales[x * gy + y])
        sums[x * kpp : (x + 1) * kpp, :] = part
    values = split(sums[...])
    owner = key_slot[pl.ds(device * key_rows, key_rows), :] // own
    flags = jnp.concatenate([jnp.where(owner == x, 1.0, 0.0) for x in range(gx)], axis=0)
    rank = group_rank(flags.astype(BF16), key_rows)
    place = jnp.zeros((key_rows, LANES), F32)
    for x in range(gx):
        here = rank[x * key_rows : (x + 1) * key_rows] + float(x * kpp)
        place = place + jnp.where(owner == x, here, 0.0)
    counts = small[height - key_rows : height]
    stacked = jnp.concatenate([place, counts], axis=0)
    columns = stacked.T
    for j in range(key_rows):
        at = slice(j * LANES, (j + 1) * LANES)
        where = columns[:, j : j + 1].astype(jnp.int32)
        hot = onehot(where == iota((LANES, key_dev), 1))
        both = dot(hot, values)
        found = both[:, :LANES] + both[:, LANES:]
        for h in range(each):
            spot = heavy[device * each + h] - device * key_dev - j * LANES
            found = found + jnp.where(iota((LANES, LANES), 0) == spot, small[h : h + 1], 0.0)
        scale = lax.rsqrt(1.0 + columns[:, key_rows + j : key_rows + j + 1])
        value = orders[at, :].astype(F32) * found * scale
        joined[at, :] = value
        result[at, :] = value.astype(BF16)
    lines = [
        joined[pl.ds(heavy[device * each + h] - device * key_dev, 1), :] for h in range(each)
    ]
    report[...] = jnp.concatenate(lines, axis=0).astype(BF16)


def all_barrier(gx, gy, me_x, me_y):
    barrier = pltpu.get_barrier_semaphore()
    device = me_x * gy + me_y
    devices = gx * gy

    @pl.loop(1, devices)
    def _(step):
        other = lax.rem(device + step, devices)
        target = (other // gy, lax.rem(other, gy))
        pl.semaphore_signal(barrier, inc=1, device_id=target, device_id_type=MESH)

    pl.semaphore_wait(barrier, devices - 1)


def exchange(me, count, moves, address):
    for source, landing, send_sem, recv_sem, local_sem in moves:
        pltpu.make_async_copy(source(me), landing(me), local_sem).start()

    def remote(other, move):
        source, landing, send_sem, recv_sem, local_sem = move
        return pltpu.make_async_remote_copy(
            src_ref=source(other),
            dst_ref=landing(me),
            send_sem=send_sem.at[other],
            recv_sem=recv_sem.at[me],
            device_id=address(other),
            device_id_type=MESH,
        )

    def finish(other, move):
        source, landing, send_sem, recv_sem, local_sem = move
        copy = pltpu.make_async_remote_copy(
            src_ref=source(other),
            dst_ref=landing(other),
            send_sem=send_sem.at[other],
            recv_sem=recv_sem.at[other],
            device_id=address(other),
            device_id_type=MESH,
        )
        copy.wait_send()
        copy.wait_recv()

    @pl.loop(1, count)
    def _(step):
        for move in moves:
            remote(lax.rem(me + step, count), move).start()

    def end():
        @pl.loop(1, count)
        def _(step):
            for move in moves:
                finish(lax.rem(me + step, count), move)

        for source, landing, send_sem, recv_sem, local_sem in moves:
            pltpu.make_async_copy(source(me), landing(me), local_sem).wait()

    return end


def to_owners(gx, gy, send, tally, small, got, got_tally, got_small, sem_a, sem_b, sem_c, sem_d, sem_e, sem_f, local):
    me_x, me_y = lax.axis_index("gx"), lax.axis_index("gy")
    all_barrier(gx, gy, me_x, me_y)
    rows = (lambda i: send.at[i], lambda i: got.at[i], sem_a, sem_b, local.at[0])
    tallies = (lambda i: tally.at[i], lambda i: got_tally.at[i], sem_c, sem_d, local.at[1])
    end_x = exchange(me_x, gx, [rows, tallies], lambda i: (i, me_y))
    others = (lambda i: small.at[i], lambda i: got_small.at[i], sem_e, sem_f, local.at[2])
    end_all = exchange(
        me_x * gy + me_y, gx * gy, [others], lambda i: (i // gy, lax.rem(i, gy))
    )
    end_x()
    end_all()


def to_ranges(gx, gy, send, scales, tally, got, got_scales, got_tally, sem_a, sem_b, sem_c, sem_d, sem_e, sem_f, local):
    me_x, me_y = lax.axis_index("gx"), lax.axis_index("gy")
    all_barrier(gx, gy, me_x, me_y)
    rows = (
        lambda i: send.at[lax.rem(i, gy) * gx + i // gy],
        lambda i: got.at[i],
        sem_a,
        sem_b,
        local.at[0],
    )
    factors = (
        lambda i: scales.at[lax.rem(i, gy) * gx + i // gy],
        lambda i: got_scales.at[i],
        sem_e,
        sem_f,
        local.at[2],
    )
    end_all = exchange(
        me_x * gy + me_y, gx * gy, [rows, factors], lambda i: (i // gy, lax.rem(i, gy))
    )
    tallies = (lambda i: tally.at[i], lambda i: got_tally.at[i], sem_c, sem_d, local.at[1])
    end_y = exchange(me_y, gy, [tallies], lambda i: (me_x, i))
    end_y()
    end_all()


def shaped(*dims, dtype=F32):
    return jax.ShapeDtypeStruct(dims, dtype)


def body(measures, row_keys, orders, heavy_keys, key_slot):
    rows, columns = measures.shape
    gx, gy = lax.axis_size("gx"), lax.axis_size("gy")
    devices = gx * gy
    key_dev = orders.shape[0]
    key_rows = key_dev // LANES
    own = key_dev * gy
    nr = key_slot.shape[0] // LANES
    heavy = heavy_keys.shape[0]
    each = heavy // devices
    capacity = max(rows // 32, 3 * rows // (4 * gx)) // 4
    segments = gx * capacity
    cfg = dict(
        rows=rows,
        block=min(rows, 2048),
        nr=nr,
        gx=gx,
        gy=gy,
        devices=devices,
        own=own,
        kpp=key_dev // gx,
        key_rows=key_rows,
        heavy=heavy,
        heavy_each=each,
        height=-(-(each + key_rows) // 8) * 8,
        capacity=capacity,
        segments=segments,
        seg_block=512 if segments % 512 == 0 else segments,
    )
    height = cfg["height"]
    group = own // LANES
    params = pltpu.CompilerParams(vmem_limit_bytes=LIMIT)
    table = key_slot.reshape(nr, LANES)
    kpp = cfg["kpp"]
    tall = group + -(-len(pieces(capacity)) // 8) * 8
    send, tally, small = pl.pallas_call(
        functools.partial(gather_rows, cfg),
        out_shape=(
            shaped(gx, capacity, columns, dtype=jnp.int16),
            shaped(gx, tall, LANES),
            shaped(devices * height, LANES),
        ),
        in_specs=[VMEM] * 4,
        out_specs=(VMEM,) * 3,
        scratch_shapes=[pltpu.VMEM((1, rows), jnp.int32), pltpu.VMEM((segments, columns), F32)],
        compiler_params=params,
    )(measures, row_keys.reshape(1, rows), heavy_keys.reshape(heavy, 1), table)
    dma = pltpu.SemaphoreType.DMA
    got, got_tally, got_small = pl.pallas_call(
        functools.partial(to_owners, gx, gy),
        out_shape=(
            shaped(gx, capacity, columns, dtype=jnp.int16),
            shaped(gx, tall, LANES),
            shaped(devices, height, LANES),
        ),
        in_specs=[ANY] * 3,
        out_specs=(ANY,) * 3,
        scratch_shapes=[dma((gx,))] * 4 + [dma((devices,))] * 2 + [dma((3,))],
        compiler_params=pltpu.CompilerParams(collective_id=0, has_side_effects=True),
    )(send, tally, small.reshape(devices, height, LANES))
    send2, scales2, tally2 = pl.pallas_call(
        functools.partial(place_rows, cfg),
        out_shape=(
            shaped(devices, kpp, columns, dtype=jnp.int16),
            shaped(devices, 1, LANES),
            shaped(group, LANES),
        ),
        in_specs=[VMEM] * 3,
        out_specs=(VMEM,) * 3,
        scratch_shapes=[pltpu.VMEM((own, LANES), F32), pltpu.VMEM((gx * group, LANES), F32)],
        compiler_params=params,
    )(got, got_tally, table)
    got2, got_scales2, got_tally2 = pl.pallas_call(
        functools.partial(to_ranges, gx, gy),
        out_shape=(
            shaped(devices, kpp, columns, dtype=jnp.int16),
            shaped(devices, 1, LANES),
            shaped(gy, key_rows, LANES),
        ),
        in_specs=[ANY] * 3,
        out_specs=(ANY,) * 3,
        scratch_shapes=[dma((devices,))] * 2
        + [dma((gy,))] * 2
        + [dma((devices,))] * 2
        + [dma((3,))],
        compiler_params=pltpu.CompilerParams(collective_id=1, has_side_effects=True),
    )(send2, scales2, tally2.reshape(gy, key_rows, LANES))
    result, report, slot_rows = pl.pallas_call(
        functools.partial(join_rows, cfg),
        out_shape=(
            shaped(key_dev, columns, dtype=BF16),
            shaped(each, columns, dtype=BF16),
            shaped(key_rows, LANES),
        ),
        in_specs=[SMEM] + [VMEM] * 6,
        out_specs=(VMEM,) * 3,
        scratch_shapes=[pltpu.VMEM((key_dev, LANES), F32)] * 2,
        compiler_params=params,
    )(
        heavy_keys,
        got2,
        got_scales2,
        got_small.reshape(devices * height, LANES),
        got_tally2.reshape(gy * key_rows, LANES),
        orders,
        table,
    )
    return (result, report, slot_rows.reshape(key_dev))


def solution(mesh):
    return jax.shard_map(
        body,
        mesh=mesh,
        in_specs=(P(("gx", "gy"), None), P(("gx", "gy")), P(("gx", "gy"), None), P(), P()),
        out_specs=(P(("gx", "gy"), None), P(("gx", "gy"), None), P(("gx", "gy"))),
        check_vma=False,
    )
```

profile of v0, /device:TPU:15, one launch (start us, length us, event | category | flops | bytes accessed | tf_op | source)
XLA Modules:
  0.0 68.7 jit_solution(13329865125586670984)
XLA Ops:
  0.6 1.4 %copy.8.heavy = s32[64,1]{1,0:T(8,128)} copy(s32[64,1]{0,1:T(1,128)} %bitcast.16) | data formatting | bytes 512 | tf_op jit(solution)/shard_map/reshape | solution.py:400
  2.0 16.3 %shard_map.76 = (s16[8,192,128]{2,1,0:T(8,128)(2,1)}, f32[8,24,128]{2,1,0:T(8,128)}, f32[256,128]{1,0:T(8,128)}) custom-call(bf16[8192,128]{1,0:T(8,128)(2,1)} %measures.1, s32[1,8192]{1,0:T(1,128)} %bitcast.13, s32[64,1]{1,0:T(8,128)} %copy.8.heavy, s32[128,128]{1,0:T(8,128)} %bitcast.8), custom_call_target="tpu_custom_call" | custom-call | tf_op jit(solution)/shard_map/pallas_call | solution.py:389
  18.3 21.3 %shard_map.77 = (s16[8,192,128]{2,1,0:T(8,128)(2,1)}, f32[8,24,128]{2,1,0:T(8,128)}, f32[32,8,128]{2,1,0:T(8,128)}) custom-call(s16[8,192,128]{2,1,0:T(8,128)(2,1)} %get-tuple-element.18.send, f32[8,24,128]{2,1,0:T(8,128)} %get-tuple-element.19.tally, f32[32,8,128]{2,1,0:T(8,128)} %bitcast.11), custom_call_target="tpu_custom_call" | custom-call | tf_op jit(solution)/shard_map/pallas_call | solution.py:402
  39.5 7.5 %shard_map.78 = (s16[32,64,128]{2,1,0:T(8,128)(2,1)}, f32[32,1,128]{2,1,0:T(1,128)}, f32[16,128]{1,0:T(8,128)}) custom-call(s16[8,192,128]{2,1,0:T(8,128)(2,1)} %get-tuple-element.21.got, f32[8,24,128]{2,1,0:T(8,128)} %get-tuple-element.22.got_tally, s32[128,128]{1,0:T(8,128)} %bitcast.9), custom_call_target="tpu_custom_call" | custom-call | tf_op jit(solution)/shard_map/pallas_call | solution.py:414
  47.0 19.1 %shard_map.79 = (s16[32,64,128]{2,1,0:T(8,128)(2,1)}, f32[32,1,128]{2,1,0:T(1,128)}, f32[4,4,128]{2,1,0:T(4,128)}) custom-call(s16[32,64,128]{2,1,0:T(8,128)(2,1)} %get-tuple-element.23.send, f32[32,1,128]{2,1,0:T(1,128)} %get-tuple-element.24.scales, f32[4,4,128]{2,1,0:T(4,128)} %bitcast.15), custom_call_target="tpu_custom_call" | custom-call | tf_op jit(solution)/shard_map/pallas_call | solution.py:426
  66.1 2.6 %shard_map.80 = (bf16[512,128]{1,0:T(8,128)(2,1)}, bf16[2,128]{1,0:T(2,128)(2,1)}, f32[4,128]{1,0:T(4,128)}) custom-call(s32[64]{0:T(128)} %heavy.1, s16[32,64,128]{2,1,0:T(8,128)(2,1)} %get-tuple-element.26.got, f32[32,1,128]{2,1,0:T(1,128)} %get-tuple-element.27.got_scales, f32[256,128]{1,0:T(8,128)} %bitcast.12, f32[16,128]{1,0:T(8,128)} %bitcast.14, ...), custom_call_target="tpu_custom_call" | custom-call | tf_op jit(solution)/shard_map/pallas_call | solution.py:441
where the time goes:
time: 68.9 us; the launch traced here: 68.7 us
  Pallas kernels  66.7 us (97%)
  local copies, waits for them, and re-layouts  1.36 us (2%)
    pallas_call x1, Pallas kernels, body(): pl.pallas_call(functools.partial(to_owners, gx, gy), out_shape=(shaped(gx...  21.3 us
    pallas_call x1, Pallas kernels, body(): pl.pallas_call(functools.partial(to_ranges, gx, gy), out_shape=(shaped(de...  19.1 us
    pallas_call x1, Pallas kernels, body(): pl.pallas_call(functools.partial(gather_rows, cfg), out_shape=(shaped(gx,...  16.3 us
    pallas_call x1, Pallas kernels, body(): pl.pallas_call(functools.partial(place_rows, cfg), out_shape=(shaped(devi...  7.48 us
    pallas_call x1, Pallas kernels, body(): pl.pallas_call(functools.partial(join_rows, cfg), out_shape=(shaped(key_d...  2.63 us

commit v1 on v0

--- a/solution.py
+++ b/solution.py
@@ -351,7 +351,7 @@
     return jax.ShapeDtypeStruct(dims, dtype)
 
 
-def body(measures, row_keys, orders, heavy_keys, key_slot):
+def split_body(measures, row_keys, orders, heavy_keys, key_slot):
     rows, columns = measures.shape
     gx, gy = lax.axis_size("gx"), lax.axis_size("gy")
     devices = gx * gy
@@ -461,6 +461,446 @@
     return (result, report, slot_rows.reshape(key_dev))
 
 
+def fused(
+    cfg, measures, keys, heavy, table,
+    got2, scales2, hgot, total_out, slot_out,
+    rows_in, seg_hot, group_row, local_row, hist, hist16, send1, got1, goth, cnt_got,
+    codes, ranks, found, wide, hsend, send2, srow, tsend, tgot,
+    load_sem, cs, cr, hs, hr, rs, rr, ys, yr, ss, sr, zs, zr, ts, tr, own_sem,
+):
+    gx, gy, nr, rows, block = cfg["gx"], cfg["gy"], cfg["nr"], cfg["rows"], cfg["block"]
+    devices, own, kpp, key_rows = cfg["devices"], cfg["own"], cfg["kpp"], cfg["key_rows"]
+    cap, extra, seg, deep = cfg["cap"], cfg["extra"], cfg["seg"], cfg["deep"]
+    each, planes = cfg["each"], cfg["planes"]
+    key_dev = key_rows * LANES
+    per_tile = LANES // kpp
+    mx, my = lax.axis_index("gx"), lax.axis_index("gy")
+    me = mx * gy + my
+    z, j = me // gx, lax.rem(me, gx)
+
+    def mesh_id(d):
+        return (d // gy, lax.rem(d, gy))
+
+    def remote(src, dst, send_sem, recv_sem, d):
+        return pltpu.make_async_remote_copy(
+            src_ref=src, dst_ref=dst, send_sem=send_sem, recv_sem=recv_sem,
+            device_id=mesh_id(d), device_id_type=MESH,
+        )
+
+    barrier = pltpu.get_barrier_semaphore()
+
+    @pl.loop(1, devices)
+    def _(step):
+        pl.semaphore_signal(
+            barrier, inc=1, device_id=mesh_id(lax.rem(me + step, devices)), device_id_type=MESH
+        )
+
+    load = pltpu.make_async_copy(measures, rows_in, load_sem)
+    load.start()
+
+    total = jnp.zeros((nr, LANES), F32)
+    for c in range(rows // block):
+        span = slice(c * block, (c + 1) * block)
+        key = keys[:, span]
+        row_hot = onehot(iota((nr, block), 0) == key >> 7)
+        seg_hot[:, span] = row_hot
+        total = total + dot(row_hot, onehot(iota((LANES, block), 0) == (key & 127)), NT)
+    hist[...] = total.reshape(devices, key_rows, LANES)
+    hist16[...] = total.astype(jnp.int32).astype(jnp.int16)
+    cnt_got[me] = hist[me]
+
+    pl.semaphore_wait(barrier, devices - 1)
+
+    @pl.loop(0, gx - 1)
+    def _(s):
+        x = lax.rem(j + 1 + s, gx)
+        t = lax.rem(2 * gx - 2 - s, gx)
+        remote(hist16, goth.at[t], hs.at[s], hr.at[t], z * gx + x).start()
+
+    @pl.loop(1, devices)
+    def _(s):
+        d = lax.rem(me + s, devices)
+        remote(hist.at[d], cnt_got.at[me], cs.at[d], cr.at[me], d).start()
+
+    owner = table[...] // own
+    heavy_key = heavy[...]
+    heads = heavy_key.shape[1]
+    code = iota((1, heads), 1) + 1
+    row_of = iota((nr, heads), 0) == heavy_key >> 7
+    col_of = onehot(iota((LANES, heads), 0) == (heavy_key & 127))
+    low = dot(jnp.where(row_of, (code & 127).astype(F32), 0.0).astype(BF16), col_of, NT)
+    high = dot(jnp.where(row_of, (code >> 7).astype(F32), 0.0).astype(BF16), col_of, NT)
+    which = (low + 128.0 * high).astype(jnp.int32)
+    codes[...] = which.astype(F32).reshape(devices, key_rows, LANES)
+    light = which == 0
+    present = (total > 0.0) & light
+    lane_r, lane_c = iota((LANES, 2 * LANES), 0), iota((LANES, 2 * LANES), 1)
+    upper = onehot((lane_c >= LANES) | (lane_r < lane_c))
+    lower = onehot(iota((nr, nr), 1) < iota((nr, nr), 0))
+    flags = jnp.concatenate(
+        [jnp.where(present & (owner == x), 1.0, 0.0) for x in range(gx)], axis=0
+    ).astype(BF16)
+    both = dot(flags, upper)
+    local = jnp.zeros((nr, LANES), F32)
+    for x in range(gx):
+        part = both[x * nr : (x + 1) * nr]
+        rank = part[:, :LANES] + dot(lower, part[:, LANES:].astype(BF16))
+        local = local + jnp.where(owner == x, rank, 0.0)
+    head = which - 1
+    block_of = head // each
+    group = jnp.where(light, owner, lax.rem(block_of, gx))
+    local = jnp.where(
+        light, local, (cap + (block_of // gx) * each + lax.rem(head, each)).astype(F32)
+    )
+    tables = jnp.concatenate([group.astype(F32).T, local.T], axis=0).astype(BF16)
+    for c in range(rows // block):
+        span = slice(c * block, (c + 1) * block)
+        spread = dot(tables, seg_hot[:, span])
+        mask = iota((LANES, block), 0) == (keys[:, span] & 127)
+        group_row[:, span] = jnp.sum(
+            jnp.where(mask, spread[:LANES], 0.0), axis=0, keepdims=True
+        ).astype(jnp.int32)
+        local_row[:, span] = jnp.sum(
+            jnp.where(mask, spread[LANES:], 0.0), axis=0, keepdims=True
+        ).astype(jnp.int32)
+
+    load.wait()
+    shifts = seg - cap - extra
+
+    def encode(values):
+        largest = jnp.max(jnp.abs(values), axis=1, keepdims=True)
+        power = jnp.floor(jnp.log2(jnp.maximum(largest, 1e-30))) + 1.0
+        fixed = jnp.clip(jnp.round(values * jnp.exp2(15.0 - power)), -32767.0, 32767.0)
+        return fixed, power
+
+    @pl.loop(0, gx)
+    def _(s):
+        x = lax.rem(j + 1 + s, gx)
+        acc = jnp.zeros((seg, LANES), F32)
+        for c in range(rows // block):
+            span = slice(c * block, (c + 1) * block)
+            place = jnp.where(group_row[:, span] == x, local_row[:, span], -1)
+            acc = acc + dot(onehot(iota((seg, block), 0) == place), rows_in[span, :])
+        fixed, power = encode(acc)
+        lines = []
+        for at, size in pieces(cap + extra):
+            diagonal = iota((size, LANES), 0) == iota((size, LANES), 1)
+            lines.append(
+                jnp.sum(jnp.where(diagonal, power[at : at + size], 0.0), axis=0, keepdims=True)
+            )
+        lines.append(jnp.zeros((shifts - len(lines), LANES), F32))
+        whole = jnp.concatenate([fixed[: cap + extra]] + lines, axis=0)
+        send1[s] = whole.astype(jnp.int32).astype(jnp.int16)
+
+        @pl.when(s < gx - 1)
+        def _():
+            t = lax.rem(2 * gx - 2 - s, gx)
+            remote(send1.at[s], got1.at[t], rs.at[s], rr.at[t], z * gx + x).start()
+
+    for t in range(gx - 1):
+        remote(hist16, goth.at[t], hs.at[gx - 2 - t], hr.at[t], me).wait_recv()
+    mine = (owner == j) & light
+    arrived = []
+    for t in range(gx):
+        here = hist16[...] if t == gx - 1 else goth[t]
+        arrived.append(jnp.where((here.astype(jnp.int32) > 0) & mine, 1.0, 0.0))
+    flags = jnp.concatenate(arrived, axis=0)
+    both = dot(flags.astype(BF16), upper)
+    for t in range(gx):
+        part = both[t * nr : (t + 1) * nr]
+        rank = part[:, :LANES] + dot(lower, part[:, LANES:].astype(BF16)) + 1.0
+        ranks[t * nr : (t + 1) * nr, :] = rank * flags[t * nr : (t + 1) * nr]
+    own_flags = onehot(owner == j)
+    both = dot(own_flags, upper)
+    row_r, row_c = iota((nr, nr), 0), iota((nr, nr), 1)
+    near = onehot((row_c < row_r) & (row_r // key_rows == row_c // key_rows))
+    rank = both[:, :LANES] + dot(near, both[:, LANES:].astype(BF16))
+    rank = jnp.where(owner == j, rank, -1.0).astype(jnp.int32)
+    for d in range(devices):
+        hot, tall = [], []
+        for q in range(key_rows):
+            r = d * key_rows + q
+            hot.append(onehot(iota((kpp, LANES), 0) == rank[r : r + 1]))
+            tall.append(ranks[pl.ds(r, gx, stride=nr), :].astype(BF16))
+        found[d * kpp : (d + 1) * kpp, 0:gx] = dot(
+            jnp.concatenate(hot, axis=1), jnp.concatenate(tall, axis=1), NT
+        )
+
+    @pl.loop(1, devices)
+    def _(s):
+        d = lax.rem(me + s, devices)
+        remote(hist.at[d], cnt_got.at[d], cs.at[d], cr.at[d], d).wait()
+
+    counted = cnt_got[0]
+    for d in range(1, devices):
+        counted = counted + cnt_got[d]
+    total_out[...] = counted
+    tsend[...] = jnp.where(codes[me] == 0.0, counted, 0.0)
+    tgot[mx] = tsend[...]
+
+    @pl.loop(1, gx)
+    def _(s):
+        x = lax.rem(mx + s, gx)
+        remote(tsend, tgot.at[mx], ts.at[x], tr.at[mx], x * gy + my).start()
+
+    heads_sum = jnp.zeros((extra, LANES), F32)
+    powers = []
+    for t in range(gx):
+        if t < gx - 1:
+            remote(send1.at[t], got1.at[t], rs.at[gx - 2 - t], rr.at[t], me).wait_recv()
+            block16 = got1[t]
+        else:
+            block16 = send1[t]
+        value = block16.astype(jnp.int32)
+        wide[t, 0:seg, :LANES] = (value >> 8).astype(F32).astype(BF16)
+        wide[t, 0:seg, LANES:] = (value & 255).astype(F32).astype(BF16)
+        if deep > seg:
+            wide[t, seg:deep, :] = jnp.zeros((deep - seg, 2 * LANES), BF16)
+        scale = jnp.exp2(value[cap + extra :].astype(F32) - 15.0)
+        line = jnp.concatenate(
+            [scale[p : p + 1] for p in range(deep // LANES)], axis=1
+        )
+        powers.append(line)
+        p, at = cap // LANES, cap % LANES
+        column = jnp.sum(
+            jnp.where(iota((extra, LANES), 1) == iota((extra, LANES), 0) + at, scale[p : p + 1], 0.0),
+            axis=1, keepdims=True,
+        )
+        heads_sum = heads_sum + value[cap : cap + extra].astype(F32) * column
+    hsend[...] = heads_sum
+
+    local_heads = pltpu.make_async_copy(hsend, hgot.at[z], own_sem.at[0])
+    local_heads.start()
+
+    @pl.loop(1, planes)
+    def _(s):
+        other = lax.rem(z + s, planes)
+        remote(hsend, hgot.at[z], zs.at[other], zr.at[z], other * gx + j).start()
+
+    chunk = gx * kpp
+    shift = lax.rem(j, per_tile) * kpp
+    half = planes // 2
+    if planes == 4:
+        order = [
+            lax.rem(z + half, planes), planes - 1 - z,
+            planes - 1 - lax.rem(z + half, planes), z,
+        ]
+    else:
+        order = [lax.rem(z + s, planes) for s in range(1, planes + 1)]
+    for c in range(planes):
+        far = order[c]
+        spot = found[pl.ds(pl.multiple_of(far * chunk, chunk), chunk), :]
+        acc = jnp.zeros((chunk, 2 * LANES), F32)
+        for t in range(gx):
+            hit = spot[:, t : t + 1].astype(jnp.int32) == iota((chunk, deep), 1) + 1
+            acc = acc + dot(jnp.where(hit, powers[t], 0.0).astype(BF16), wide[t])
+        fixed, power = encode(acc[:, :LANES] * 256.0 + acc[:, LANES:])
+        send2[c] = fixed.astype(jnp.int32).astype(jnp.int16).reshape(gx, kpp, LANES)
+        scale = jnp.exp2(power - 15.0)
+        diagonal = iota((kpp, LANES), 1) == iota((kpp, LANES), 0) + shift
+        for x in range(gx):
+            srow[c, x] = jnp.sum(
+                jnp.where(diagonal, scale[x * kpp : (x + 1) * kpp], 0.0), axis=0, keepdims=True
+            )
+        last = c == planes - 1
+
+        @pl.loop(0, gx - 1 if last else gx)
+        def _(s):
+            x = lax.rem(j + 1 + s, gx)
+            d = far * gx + x
+            remote(send2.at[c, x], got2.at[me], ys.at[d], yr.at[me], d).start()
+            remote(srow.at[c, x], scales2.at[me], ss.at[d], sr.at[me], d).start()
+
+        if last:
+            keep = pltpu.make_async_copy(send2.at[c, j], got2.at[me], own_sem.at[1])
+            keep.start()
+            keep_row = pltpu.make_async_copy(srow.at[c, j], scales2.at[me], own_sem.at[2])
+            keep_row.start()
+
+    @pl.loop(1, gx)
+    def _(s):
+        x = lax.rem(mx + s, gx)
+        remote(tsend, tgot.at[x], ts.at[x], tr.at[x], x * gy + my).wait()
+
+    base = me * key_dev
+    left, right = [], []
+    for m in range(gx):
+        slots = table[pl.ds((m * gy + my) * key_rows, key_rows), :] - base
+        for q in range(key_rows):
+            line = slots[q : q + 1]
+            amount = tgot[m, q : q + 1, :].astype(jnp.int32)
+            bands = [
+                jnp.where(
+                    iota((8, LANES), 0) == (line >> 7), ((amount >> (8 * b)) & 255).astype(F32), 0.0
+                )
+                for b in range(3)
+            ]
+            left.append(jnp.concatenate(bands + [jnp.zeros((8, LANES), F32)], axis=0).astype(BF16))
+            right.append(onehot(iota((LANES, LANES), 0) == (line & 127)))
+    bands = dot(jnp.concatenate(left, axis=1), jnp.concatenate(right, axis=1), NT)
+    slot_out[...] = (bands[0:8] + 256.0 * bands[8:16] + 65536.0 * bands[16:24])[0:key_rows]
+
+    for s in range(gx - 1):
+        t = (2 * gx - 2 - s) % gx
+        remote(hist16, goth.at[t], hs.at[s], hr.at[t], me).wait_send()
+        remote(send1.at[s], got1.at[t], rs.at[s], rr.at[t], me).wait_send()
+    local_heads.wait()
+    keep.wait()
+    keep_row.wait()
+
+    @pl.loop(1, planes)
+    def _(s):
+        other = lax.rem(z + s, planes)
+        remote(hsend, hgot.at[other], zs.at[other], zr.at[other], other * gx + j).wait()
+
+    @pl.loop(1, devices)
+    def _(s):
+        d = lax.rem(me + s, devices)
+        remote(send2.at[0, 0], got2.at[d], ys.at[d], yr.at[d], d).wait()
+        remote(srow.at[0, 0], scales2.at[d], ss.at[d], sr.at[d], d).wait()
+
+
+def join(cfg, heavy, got, scales, heads, total, slot_in, orders, table, result, report, slot_rows, joined):
+    gx, gy, own, kpp = cfg["gx"], cfg["gy"], cfg["own"], cfg["kpp"]
+    key_rows, each, planes, extra = cfg["key_rows"], cfg["each"], cfg["planes"], cfg["extra"]
+    key_dev = key_rows * LANES
+    per_tile = LANES // kpp
+    device = lax.axis_index("gx") * gy + lax.axis_index("gy")
+    slot_rows[...] = slot_in[...]
+    z = device // gx
+    small = heads[0]
+    for p in range(1, planes):
+        small = small + heads[p]
+    owner = table[pl.ds(device * key_rows, key_rows), :] // own
+    flags = jnp.concatenate([jnp.where(owner == x, 1.0, 0.0) for x in range(gx)], axis=0)
+    rank = group_rank(flags.astype(BF16), key_rows)
+    place = jnp.zeros((key_rows, LANES), F32)
+    for x in range(gx):
+        here = rank[x * key_rows : (x + 1) * key_rows] + float(x * kpp)
+        place = place + jnp.where(owner == x, here, 0.0)
+    columns = jnp.concatenate([place, total[...]], axis=0).T
+    values, lines = [], []
+    for p in range(planes):
+        value = got[p * gx : (p + 1) * gx].reshape(key_dev, LANES).astype(jnp.int32)
+        values.append(
+            jnp.concatenate([(value >> 8).astype(F32), (value & 255).astype(F32)], axis=1).astype(BF16)
+        )
+        tiles = []
+        for x in range(0, gx, per_tile):
+            tile = scales[p * gx + x]
+            for i in range(1, per_tile):
+                tile = tile + scales[p * gx + x + i]
+            tiles.append(tile)
+        lines.append(jnp.concatenate(tiles, axis=1))
+    for j in range(key_rows):
+        at = slice(j * LANES, (j + 1) * LANES)
+        hit = columns[:, j : j + 1].astype(jnp.int32) == iota((LANES, key_dev), 1)
+        both = jnp.zeros((LANES, 2 * LANES), F32)
+        for p in range(planes):
+            both = both + dot(jnp.where(hit, lines[p], 0.0).astype(BF16), values[p])
+        sums = both[:, :LANES] * 256.0 + both[:, LANES:]
+        for h in range(each):
+            spot = heavy[device * each + h] - device * key_dev - j * LANES
+            line = jnp.sum(
+                jnp.where(iota((extra, LANES), 0) == z * each + h, small, 0.0), axis=0, keepdims=True
+            )
+            sums = sums + jnp.where(iota((LANES, LANES), 0) == spot, line, 0.0)
+        scale = lax.rsqrt(1.0 + columns[:, key_rows + j : key_rows + j + 1])
+        value = orders[at, :].astype(F32) * sums * scale
+        joined[at, :] = value
+        result[at, :] = value.astype(BF16)
+    picked = [
+        joined[pl.ds(heavy[device * each + h] - device * key_dev, 1), :] for h in range(each)
+    ]
+    report[...] = jnp.concatenate(picked, axis=0).astype(BF16)
+
+
+def body(measures, row_keys, orders, heavy_keys, key_slot):
+    rows, columns = measures.shape
+    gx, gy = lax.axis_size("gx"), lax.axis_size("gy")
+    devices = gx * gy
+    key_dev = orders.shape[0]
+    key_rows = key_dev // LANES
+    nr = key_slot.shape[0] // LANES
+    heavy = heavy_keys.shape[0]
+    each = heavy // devices
+    if gx * nr > 2048:
+        return split_body(measures, row_keys, orders, heavy_keys, key_slot)
+    planes = devices // gx
+    cap = max(rows // 32, 3 * rows // (4 * gx)) // 4
+    extra = planes * each
+    seg = -(-(cap + extra + len(pieces(cap + extra))) // 16) * 16
+    deep = -(-cap // LANES) * LANES
+    kpp = key_dev // gx
+    cfg = dict(
+        rows=rows, block=min(rows, 2048), nr=nr, gx=gx, gy=gy, devices=devices,
+        own=key_dev * gy, kpp=kpp, key_rows=key_rows, each=each, planes=planes,
+        cap=cap, extra=extra, seg=seg, deep=max(deep, -(-seg // LANES) * LANES),
+    )
+    deep = cfg["deep"]
+    table = key_slot.reshape(nr, LANES)
+    dma = pltpu.SemaphoreType.DMA
+    i16 = jnp.int16
+    got, scales, heads, total, slots = pl.pallas_call(
+        functools.partial(fused, cfg),
+        out_shape=(
+            shaped(devices, kpp, columns, dtype=i16),
+            shaped(devices, 1, LANES),
+            shaped(planes, extra, LANES),
+            shaped(key_rows, LANES),
+            shaped(key_rows, LANES),
+        ),
+        in_specs=[ANY] + [VMEM] * 3,
+        out_specs=(ANY,) * 3 + (VMEM,) * 2,
+        scratch_shapes=[
+            pltpu.VMEM((rows, columns), BF16),
+            pltpu.VMEM((nr, rows), BF16),
+            pltpu.VMEM((1, rows), jnp.int32),
+            pltpu.VMEM((1, rows), jnp.int32),
+            pltpu.VMEM((devices, key_rows, LANES), F32),
+            pltpu.VMEM((nr, LANES), i16),
+            pltpu.VMEM((gx, seg, LANES), i16),
+            pltpu.VMEM((gx, seg, LANES), i16),
+            pltpu.VMEM((gx, nr, LANES), i16),
+            pltpu.VMEM((devices, key_rows, LANES), F32),
+            pltpu.VMEM((devices, key_rows, LANES), F32),
+            pltpu.VMEM((gx * nr, LANES), F32),
+            pltpu.VMEM((devices * kpp, LANES), F32),
+            pltpu.VMEM((gx, deep, 2 * LANES), BF16),
+            pltpu.VMEM((extra, LANES), F32),
+            pltpu.VMEM((planes, gx, kpp, LANES), i16),
+            pltpu.VMEM((planes, gx, 1, LANES), F32),
+            pltpu.VMEM((key_rows, LANES), F32),
+            pltpu.VMEM((gx, key_rows, LANES), F32),
+            dma,
+            dma((devices,)), dma((devices,)),
+            dma((gx,)), dma((gx,)),
+            dma((gx,)), dma((gx,)),
+            dma((devices,)), dma((devices,)),
+            dma((devices,)), dma((devices,)),
+            dma((planes,)), dma((planes,)),
+            dma((gx,)), dma((gx,)),
+            dma((3,)),
+        ],
+        compiler_params=pltpu.CompilerParams(
+            collective_id=2, has_side_effects=True, vmem_limit_bytes=LIMIT
+        ),
+    )(measures, row_keys.reshape(1, rows), heavy_keys.reshape(1, heavy), table)
+    result, report, slot_rows = pl.pallas_call(
+        functools.partial(join, cfg),
+        out_shape=(
+            shaped(key_dev, columns, dtype=BF16),
+            shaped(each, columns, dtype=BF16),
+            shaped(key_rows, LANES),
+        ),
+        in_specs=[SMEM] + [VMEM] * 7,
+        out_specs=(VMEM,) * 3,
+        scratch_shapes=[pltpu.VMEM((key_dev, LANES), F32)],
+        compiler_params=pltpu.CompilerParams(vmem_limit_bytes=LIMIT),
+    )(heavy_keys, got, scales, heads, total, slots, orders, table)
+    return (result, report, slot_rows.reshape(key_dev))
+
+
 def solution(mesh):
     return jax.shard_map(
         body,

time: 68.9 us -> 43.9 us (0.64)
  the two profiles are of different devices: /device:TPU:15 before, /device:TPU:0 now
where the time goes in v1:
time: 43.9 us; the launch traced here: 43.7 us
  Pallas kernels  43.1 us (98%)
  between operations  0.64 us (1%)
    pallas_call x1, Pallas kernels, body(): pl.pallas_call(functools.partial(fused, cfg), out_shape=(shaped(devices,...  40.1 us
    pallas_call x1, Pallas kernels, body(): pl.pallas_call(functools.partial(join, cfg), out_shape=(shaped(key_dev, c...  2.99 us

profile of v1, /device:TPU:0, one launch (start us, length us, event | category | flops | bytes accessed | tf_op | source)
XLA Modules:
  0.0 43.7 jit_solution(10279391193791502952)
XLA Ops:
  0.6 40.1 %shard_map.76 = (s16[32,64,128]{2,1,0:T(8,128)(2,1)}, f32[32,1,128]{2,1,0:T(1,128)}, f32[4,8,128]{2,1,0:T(8,128)}, f32[4,128]{1,0:T(4,128)}, f32[4,128]{1,0:T(4,128)}) custom-call(bf16[8192,128]{1,0:T(8,128)(2,1)} %measures.1, s32[1,8192]{1,0:T(1,128)} %bitcast.6, s32[1,64]{1,0:T(1,128)} %bitcast.7, s32[128,128]{1,0:T(8,128)} %bitcast.4), custom_call_target="tpu_custom_call" | custom-call | tf_op jit(solution)/shard_map/pallas_call | solution.py:844
  40.7 3.0 %shard_map.77 = (bf16[512,128]{1,0:T(8,128)(2,1)}, bf16[2,128]{1,0:T(2,128)(2,1)}, f32[4,128]{1,0:T(4,128)}) custom-call(s32[64]{0:T(128)} %heavy.1, s16[32,64,128]{2,1,0:T(8,128)(2,1)} %get-tuple-element.11.got, f32[32,1,128]{2,1,0:T(1,128)} %get-tuple-element.12.scales, f32[4,8,128]{2,1,0:T(8,128)} %get-tuple-element.13.heads, ...), custom_call_target="tpu_custom_call" | custom-call | tf_op jit(solution)/shard_map/pallas_call | solution.py:889

commit v2 on v1

--- a/solution.py
+++ b/solution.py
@@ -9,6 +9,7 @@
 
 MESH = pl.DeviceIdType.MESH
 LANES = 128
+LEAST = -3.4028235e38
 F32 = jnp.float32
 BF16 = jnp.bfloat16
 VMEM = pl.BlockSpec(memory_space=pltpu.VMEM)
@@ -61,6 +62,10 @@
 def decode(fixed, scale):
     column = jnp.sum(jnp.where(eye(fixed.shape[0]), scale, 0.0), axis=1, keepdims=True)
     return fixed.astype(jnp.int32).astype(F32) * (column * (1.0 / 32767.0))
+
+
+def joined_chains(chains):
+    return chains[0] + jnp.maximum(chains[1], LEAST)
 
 
 def pieces(total):
@@ -462,65 +467,82 @@
 
 
 def fused(
-    cfg, measures, keys, heavy, table,
-    got2, scales2, hgot, total_out, slot_out,
-    rows_in, seg_hot, group_row, local_row, hist, hist16, send1, got1, goth, cnt_got,
+    cfg, measures, keys_hbm, heavy_hbm, table_hbm,
+    got2, scales2, hgot, side_out,
+    keys, heavy, table, side, rows_in, pair, parity, seg_hot, group_row, local_row, hist, hist16, send1, got1, goth, cnt_got,
     codes, ranks, found, wide, hsend, send2, srow, tsend, tgot,
-    load_sem, cs, cr, hs, hr, rs, rr, ys, yr, ss, sr, zs, zr, ts, tr, own_sem,
+    load_sem, in_sem, out_sem, back_sem, row_sem, own_sem,
 ):
     gx, gy, nr, rows, block = cfg["gx"], cfg["gy"], cfg["nr"], cfg["rows"], cfg["block"]
     devices, own, kpp, key_rows = cfg["devices"], cfg["own"], cfg["kpp"], cfg["key_rows"]
     cap, extra, seg, deep = cfg["cap"], cfg["extra"], cfg["seg"], cfg["deep"]
-    each, planes = cfg["each"], cfg["planes"]
+    each, planes, half_seg = cfg["each"], cfg["planes"], cfg["seg"] // 2
+    used, at_once = (cap + extra) // 2, cfg["at_once"]
     key_dev = key_rows * LANES
     per_tile = LANES // kpp
     mx, my = lax.axis_index("gx"), lax.axis_index("gy")
     me = mx * gy + my
     z, j = me // gx, lax.rem(me, gx)
 
-    def mesh_id(d):
-        return (d // gy, lax.rem(d, gy))
-
-    def remote(src, dst, send_sem, recv_sem, d):
+    def remote(src, dst, send_sem, recv_sem, where):
         return pltpu.make_async_remote_copy(
             src_ref=src, dst_ref=dst, send_sem=send_sem, recv_sem=recv_sem,
-            device_id=mesh_id(d), device_id_type=MESH,
+            device_id=where, device_id_type=MESH,
         )
 
-    barrier = pltpu.get_barrier_semaphore()
-
-    @pl.loop(1, devices)
-    def _(step):
-        pl.semaphore_signal(
-            barrier, inc=1, device_id=mesh_id(lax.rem(me + step, devices)), device_id_type=MESH
+    def in_plane(p, x):
+        d = p * gx + x
+        return (d // gy, lax.rem(d, gy))
+
+    beside = [lax.rem(my + s, gy) for s in range(gy)]
+
+    def every_other(act):
+        for y in beside[1:]:
+            act(mx * gy + y, (mx, y))
+
+        @pl.loop(1, gx)
+        def _(s):
+            x = lax.rem(mx + s, gx)
+            for y in beside:
+                act(x * gy + y, (x, y))
+
+    self_id = (mx, my)
+    others = devices - 1
+    COUNTS, HISTS, ROWS, MERGED, SCALES, HEADS, TOTALS = range(7)
+
+    loads = [
+        pltpu.make_async_copy(source, target, in_sem.at[i])
+        for i, (source, target) in enumerate(
+            [(keys_hbm, keys), (heavy_hbm, heavy), (table_hbm, table)]
         )
-
+    ]
+    for one in loads:
+        one.start()
     load = pltpu.make_async_copy(measures, rows_in, load_sem)
     load.start()
 
-    total = jnp.zeros((nr, LANES), F32)
+    barrier = pltpu.get_barrier_semaphore()
+
+    every_other(
+        lambda d, where: pl.semaphore_signal(
+            barrier, inc=1, device_id=where, device_id_type=MESH
+        )
+    )
+    for one in loads:
+        one.wait()
+
+    chains = [jnp.zeros((nr, LANES), F32)] * 2
     for c in range(rows // block):
         span = slice(c * block, (c + 1) * block)
         key = keys[:, span]
         row_hot = onehot(iota((nr, block), 0) == key >> 7)
         seg_hot[:, span] = row_hot
-        total = total + dot(row_hot, onehot(iota((LANES, block), 0) == (key & 127)), NT)
+        column_hot = onehot(iota((LANES, block), 0) == (key & 127))
+        chains[c % 2] = chains[c % 2] + dot(row_hot, column_hot, NT)
+    total = joined_chains(chains)
     hist[...] = total.reshape(devices, key_rows, LANES)
     hist16[...] = total.astype(jnp.int32).astype(jnp.int16)
     cnt_got[me] = hist[me]
-
-    pl.semaphore_wait(barrier, devices - 1)
-
-    @pl.loop(0, gx - 1)
-    def _(s):
-        x = lax.rem(j + 1 + s, gx)
-        t = lax.rem(2 * gx - 2 - s, gx)
-        remote(hist16, goth.at[t], hs.at[s], hr.at[t], z * gx + x).start()
-
-    @pl.loop(1, devices)
-    def _(s):
-        d = lax.rem(me + s, devices)
-        remote(hist.at[d], cnt_got.at[me], cs.at[d], cr.at[me], d).start()
 
     owner = table[...] // own
     heavy_key = heavy[...]
@@ -560,12 +582,37 @@
         group_row[:, span] = jnp.sum(
             jnp.where(mask, spread[:LANES], 0.0), axis=0, keepdims=True
         ).astype(jnp.int32)
-        local_row[:, span] = jnp.sum(
+        inside = jnp.sum(
             jnp.where(mask, spread[LANES:], 0.0), axis=0, keepdims=True
         ).astype(jnp.int32)
+        local_row[:, span] = inside >> 1
+        odd = (inside & 1).astype(F32)
+        for i in range(block // LANES):
+            at = c * (block // LANES) + i
+            parity[at : at + 1, :] = odd[:, i * LANES : (i + 1) * LANES]
+
+    pl.semaphore_wait(barrier, devices - 1)
+
+    @pl.loop(0, gx - 1)
+    def _(s):
+        x = lax.rem(j + 1 + s, gx)
+        t = lax.rem(2 * gx - 2 - s, gx)
+        remote(hist16, goth.at[t], out_sem.at[HISTS], back_sem.at[HISTS], in_plane(z, x)).start()
+
+    every_other(
+        lambda d, where: remote(
+            hist.at[d], cnt_got.at[me], out_sem.at[COUNTS], back_sem.at[COUNTS], where
+        ).start()
+    )
 
     load.wait()
-    shifts = seg - cap - extra
+    turned = parity[...].T
+    for c in range(rows // LANES):
+        span = slice(c * LANES, (c + 1) * LANES)
+        line = rows_in[span, :]
+        odd = line * jnp.broadcast_to(turned[:, c : c + 1], (LANES, LANES)).astype(BF16)
+        pair[span, LANES:] = odd
+        pair[span, :LANES] = line - odd
 
     def encode(values):
         largest = jnp.max(jnp.abs(values), axis=1, keepdims=True)
@@ -573,32 +620,53 @@
         fixed = jnp.clip(jnp.round(values * jnp.exp2(15.0 - power)), -32767.0, 32767.0)
         return fixed, power
 
-    @pl.loop(0, gx)
-    def _(s):
-        x = lax.rem(j + 1 + s, gx)
-        acc = jnp.zeros((seg, LANES), F32)
+    for first in range(0, gx, at_once):
+        steps = range(first, first + at_once)
+        chains = [jnp.zeros((at_once * half_seg, 2 * LANES), F32)] * 2
         for c in range(rows // block):
             span = slice(c * block, (c + 1) * block)
-            place = jnp.where(group_row[:, span] == x, local_row[:, span], -1)
-            acc = acc + dot(onehot(iota((seg, block), 0) == place), rows_in[span, :])
-        fixed, power = encode(acc)
-        lines = []
-        for at, size in pieces(cap + extra):
-            diagonal = iota((size, LANES), 0) == iota((size, LANES), 1)
-            lines.append(
-                jnp.sum(jnp.where(diagonal, power[at : at + size], 0.0), axis=0, keepdims=True)
+            group, local = group_row[:, span], local_row[:, span]
+            hot = [
+                jnp.where(
+                    iota((half_seg, block), 0)
+                    == jnp.where(group == lax.rem(j + 1 + s, gx), local, -1),
+                    1.0,
+                    0.0,
+                )
+                for s in steps
+            ]
+            chains[c % 2] = chains[c % 2] + dot(
+                jnp.concatenate(hot, axis=0).astype(BF16), pair[span, :]
             )
-        lines.append(jnp.zeros((shifts - len(lines), LANES), F32))
-        whole = jnp.concatenate([fixed[: cap + extra]] + lines, axis=0)
-        send1[s] = whole.astype(jnp.int32).astype(jnp.int16)
-
-        @pl.when(s < gx - 1)
-        def _():
-            t = lax.rem(2 * gx - 2 - s, gx)
-            remote(send1.at[s], got1.at[t], rs.at[s], rr.at[t], z * gx + x).start()
-
-    for t in range(gx - 1):
-        remote(hist16, goth.at[t], hs.at[gx - 2 - t], hr.at[t], me).wait_recv()
+        acc = joined_chains(chains)
+        for s in steps:
+            at = (s - first) * half_seg
+            both = acc[at : at + half_seg]
+            fixed, power = encode(jnp.concatenate([both[:, :LANES], both[:, LANES:]], axis=0))
+            lines = []
+            for top, size in pieces(seg):
+                diagonal = iota((size, LANES), 0) == iota((size, LANES), 1)
+                lines.append(
+                    jnp.sum(jnp.where(diagonal, power[top : top + size], 0.0), axis=0, keepdims=True)
+                )
+            foot = jnp.zeros((half_seg - used, LANES), F32)
+            for n, one in enumerate(lines):
+                foot = jnp.where(iota(foot.shape, 0) == n, one, foot)
+            whole = jnp.concatenate([fixed[:used], foot, fixed[half_seg:]], axis=0)
+            send1[s] = whole.astype(jnp.int32).astype(jnp.int16)
+            if s < gx - 1:
+                t = (2 * gx - 2 - s) % gx
+                remote(
+                    send1.at[s], got1.at[t], out_sem.at[ROWS], row_sem.at[t],
+                    in_plane(z, lax.rem(j + 1 + s, gx)),
+                ).start()
+
+    def all_of(ref, kind, number):
+        return remote(
+            ref.at[0:number], ref.at[0:number], out_sem.at[kind], back_sem.at[kind], self_id
+        )
+
+    all_of(goth, HISTS, gx - 1).wait_recv()
     mine = (owner == j) & light
     arrived = []
     for t in range(gx):
@@ -608,7 +676,8 @@
     both = dot(flags.astype(BF16), upper)
     for t in range(gx):
         part = both[t * nr : (t + 1) * nr]
-        rank = part[:, :LANES] + dot(lower, part[:, LANES:].astype(BF16)) + 1.0
+        rank = (part[:, :LANES] + dot(lower, part[:, LANES:].astype(BF16))).astype(jnp.int32)
+        rank = ((rank >> 1) + (rank & 1) * half_seg + 1).astype(F32)
         ranks[t * nr : (t + 1) * nr, :] = rank * flags[t * nr : (t + 1) * nr]
     own_flags = onehot(owner == j)
     both = dot(own_flags, upper)
@@ -626,28 +695,25 @@
             jnp.concatenate(hot, axis=1), jnp.concatenate(tall, axis=1), NT
         )
 
-    @pl.loop(1, devices)
-    def _(s):
-        d = lax.rem(me + s, devices)
-        remote(hist.at[d], cnt_got.at[d], cs.at[d], cr.at[d], d).wait()
+    all_of(cnt_got, COUNTS, others).wait()
 
     counted = cnt_got[0]
     for d in range(1, devices):
         counted = counted + cnt_got[d]
-    total_out[...] = counted
+    side[key_rows : 2 * key_rows, :] = counted
     tsend[...] = jnp.where(codes[me] == 0.0, counted, 0.0)
     tgot[mx] = tsend[...]
 
     @pl.loop(1, gx)
     def _(s):
         x = lax.rem(mx + s, gx)
-        remote(tsend, tgot.at[mx], ts.at[x], tr.at[mx], x * gy + my).start()
-
-    heads_sum = jnp.zeros((extra, LANES), F32)
+        remote(tsend, tgot.at[mx], out_sem.at[TOTALS], back_sem.at[TOTALS], (x, my)).start()
+
+    heads_sum = [jnp.zeros((extra // 2, LANES), F32)] * 2
     powers = []
     for t in range(gx):
         if t < gx - 1:
-            remote(send1.at[t], got1.at[t], rs.at[gx - 2 - t], rr.at[t], me).wait_recv()
+            remote(send1.at[t], got1.at[t], out_sem.at[ROWS], row_sem.at[t], self_id).wait_recv()
             block16 = got1[t]
         else:
             block16 = send1[t]
@@ -656,18 +722,23 @@
         wide[t, 0:seg, LANES:] = (value & 255).astype(F32).astype(BF16)
         if deep > seg:
             wide[t, seg:deep, :] = jnp.zeros((deep - seg, 2 * LANES), BF16)
-        scale = jnp.exp2(value[cap + extra :].astype(F32) - 15.0)
-        line = jnp.concatenate(
-            [scale[p : p + 1] for p in range(deep // LANES)], axis=1
+        scale = jnp.exp2(value[used : used + len(pieces(seg))].astype(F32) - 15.0)
+        powers.append(
+            jnp.concatenate([scale[p : p + 1] for p in range(deep // LANES)], axis=1)
         )
-        powers.append(line)
-        p, at = cap // LANES, cap % LANES
-        column = jnp.sum(
-            jnp.where(iota((extra, LANES), 1) == iota((extra, LANES), 0) + at, scale[p : p + 1], 0.0),
-            axis=1, keepdims=True,
-        )
-        heads_sum = heads_sum + value[cap : cap + extra].astype(F32) * column
-    hsend[...] = heads_sum
+        for b in range(2):
+            top = b * half_seg + cap // 2
+            p, at = top // LANES, top % LANES
+            column = jnp.sum(
+                jnp.where(
+                    iota((extra // 2, LANES), 1) == iota((extra // 2, LANES), 0) + at,
+                    scale[p : p + 1],
+                    0.0,
+                ),
+                axis=1, keepdims=True,
+            )
+            heads_sum[b] = heads_sum[b] + value[top : top + extra // 2].astype(F32) * column
+    hsend[...] = jnp.concatenate(heads_sum, axis=0)
 
     local_heads = pltpu.make_async_copy(hsend, hgot.at[z], own_sem.at[0])
     local_heads.start()
@@ -675,11 +746,14 @@
     @pl.loop(1, planes)
     def _(s):
         other = lax.rem(z + s, planes)
-        remote(hsend, hgot.at[z], zs.at[other], zr.at[z], other * gx + j).start()
+        remote(
+            hsend, hgot.at[z], out_sem.at[HEADS], back_sem.at[HEADS], in_plane(other, j)
+        ).start()
 
     chunk = gx * kpp
     shift = lax.rem(j, per_tile) * kpp
     half = planes // 2
+    lanes = (iota((1, deep), 1) + 1).astype(F32)
     if planes == 4:
         order = [
             lax.rem(z + half, planes), planes - 1 - z,
@@ -690,10 +764,13 @@
     for c in range(planes):
         far = order[c]
         spot = found[pl.ds(pl.multiple_of(far * chunk, chunk), chunk), :]
-        acc = jnp.zeros((chunk, 2 * LANES), F32)
+        chains = [jnp.zeros((chunk, 2 * LANES), F32)] * 2
         for t in range(gx):
-            hit = spot[:, t : t + 1].astype(jnp.int32) == iota((chunk, deep), 1) + 1
-            acc = acc + dot(jnp.where(hit, powers[t], 0.0).astype(BF16), wide[t])
+            hit = spot[:, t : t + 1] == lanes
+            chains[t % 2] = chains[t % 2] + dot(
+                jnp.where(hit, powers[t], 0.0).astype(BF16), wide[t]
+            )
+        acc = joined_chains(chains)
         fixed, power = encode(acc[:, :LANES] * 256.0 + acc[:, LANES:])
         send2[c] = fixed.astype(jnp.int32).astype(jnp.int16).reshape(gx, kpp, LANES)
         scale = jnp.exp2(power - 15.0)
@@ -707,9 +784,13 @@
         @pl.loop(0, gx - 1 if last else gx)
         def _(s):
             x = lax.rem(j + 1 + s, gx)
-            d = far * gx + x
-            remote(send2.at[c, x], got2.at[me], ys.at[d], yr.at[me], d).start()
-            remote(srow.at[c, x], scales2.at[me], ss.at[d], sr.at[me], d).start()
+            where = in_plane(far, x)
+            remote(
+                send2.at[c, x], got2.at[me], out_sem.at[MERGED], back_sem.at[MERGED], where
+            ).start()
+            remote(
+                srow.at[c, x], scales2.at[me], out_sem.at[SCALES], back_sem.at[SCALES], where
+            ).start()
 
         if last:
             keep = pltpu.make_async_copy(send2.at[c, j], got2.at[me], own_sem.at[1])
@@ -717,10 +798,7 @@
             keep_row = pltpu.make_async_copy(srow.at[c, j], scales2.at[me], own_sem.at[2])
             keep_row.start()
 
-    @pl.loop(1, gx)
-    def _(s):
-        x = lax.rem(mx + s, gx)
-        remote(tsend, tgot.at[x], ts.at[x], tr.at[x], x * gy + my).wait()
+    all_of(tgot, TOTALS, gx - 1).wait()
 
     base = me * key_dev
     left, right = [], []
@@ -737,48 +815,69 @@
             ]
             left.append(jnp.concatenate(bands + [jnp.zeros((8, LANES), F32)], axis=0).astype(BF16))
             right.append(onehot(iota((LANES, LANES), 0) == (line & 127)))
-    bands = dot(jnp.concatenate(left, axis=1), jnp.concatenate(right, axis=1), NT)
-    slot_out[...] = (bands[0:8] + 256.0 * bands[8:16] + 65536.0 * bands[16:24])[0:key_rows]
-
-    for s in range(gx - 1):
-        t = (2 * gx - 2 - s) % gx
-        remote(hist16, goth.at[t], hs.at[s], hr.at[t], me).wait_send()
-        remote(send1.at[s], got1.at[t], rs.at[s], rr.at[t], me).wait_send()
-    local_heads.wait()
-    keep.wait()
-    keep_row.wait()
-
-    @pl.loop(1, planes)
-    def _(s):
-        other = lax.rem(z + s, planes)
-        remote(hsend, hgot.at[other], zs.at[other], zr.at[other], other * gx + j).wait()
-
-    @pl.loop(1, devices)
-    def _(s):
-        d = lax.rem(me + s, devices)
-        remote(send2.at[0, 0], got2.at[d], ys.at[d], yr.at[d], d).wait()
-        remote(srow.at[0, 0], scales2.at[d], ss.at[d], sr.at[d], d).wait()
-
-
-def join(cfg, heavy, got, scales, heads, total, slot_in, orders, table, result, report, slot_rows, joined):
-    gx, gy, own, kpp = cfg["gx"], cfg["gy"], cfg["own"], cfg["kpp"]
-    key_rows, each, planes, extra = cfg["key_rows"], cfg["each"], cfg["planes"], cfg["extra"]
-    key_dev = key_rows * LANES
-    per_tile = LANES // kpp
-    device = lax.axis_index("gx") * gy + lax.axis_index("gy")
-    slot_rows[...] = slot_in[...]
-    z = device // gx
-    small = heads[0]
-    for p in range(1, planes):
-        small = small + heads[p]
-    owner = table[pl.ds(device * key_rows, key_rows), :] // own
+    middle = len(left) // 2
+    bands = joined_chains(
+        [
+            dot(jnp.concatenate(left[part], axis=1), jnp.concatenate(right[part], axis=1), NT)
+            for part in (slice(0, middle), slice(middle, None))
+        ]
+    )
+    side[2 * key_rows : 3 * key_rows, :] = (
+        bands[0:8] + 256.0 * bands[8:16] + 65536.0 * bands[16:24]
+    )[0:key_rows]
+    owner = table[pl.ds(me * key_rows, key_rows), :] // own
     flags = jnp.concatenate([jnp.where(owner == x, 1.0, 0.0) for x in range(gx)], axis=0)
     rank = group_rank(flags.astype(BF16), key_rows)
     place = jnp.zeros((key_rows, LANES), F32)
     for x in range(gx):
-        here = rank[x * key_rows : (x + 1) * key_rows] + float(x * kpp)
-        place = place + jnp.where(owner == x, here, 0.0)
-    columns = jnp.concatenate([place, total[...]], axis=0).T
+        inside = rank[x * key_rows : (x + 1) * key_rows] + float(x * kpp)
+        place = place + jnp.where(owner == x, inside, 0.0)
+    side[0:key_rows, :] = place
+    hand_over = pltpu.make_async_copy(side, side_out, own_sem.at[3])
+    hand_over.start()
+
+    all_of(goth, HISTS, gx - 1).wait_send()
+    all_of(send1, ROWS, gx - 1).wait_send()
+    local_heads.wait()
+    keep.wait()
+    keep_row.wait()
+    hand_over.wait()
+    all_of(hgot, HEADS, planes - 1).wait()
+    all_of(got2, MERGED, others).wait()
+    all_of(scales2, SCALES, others).wait()
+
+
+def join(
+    cfg, heavy, got_hbm, scales_hbm, heads_hbm, side_hbm, orders_hbm, result, report, slot_rows,
+    joined, got, scales, heads, side, orders, sems,
+):
+    gx, gy, kpp = cfg["gx"], cfg["gy"], cfg["kpp"]
+    key_rows, each, planes, extra = cfg["key_rows"], cfg["each"], cfg["planes"], cfg["extra"]
+    key_dev = key_rows * LANES
+    per_tile = LANES // kpp
+    loads = [
+        pltpu.make_async_copy(source, target, sems.at[i])
+        for i, (source, target) in enumerate(
+            [(got_hbm, got), (side_hbm, side), (scales_hbm, scales), (heads_hbm, heads), (orders_hbm, orders)]
+        )
+    ]
+    for one in loads:
+        one.start()
+    device = lax.axis_index("gx") * gy + lax.axis_index("gy")
+    z = device // gx
+    for one in loads[1:4]:
+        one.wait()
+    slot_rows[...] = side[2 * key_rows : 3 * key_rows, :]
+    small = heads[0]
+    for p in range(1, planes):
+        small = small + heads[p]
+    spots = []
+    for h in range(each):
+        entry = z * each + h
+        spots.append(lax.rem(entry, 2) * (extra // 2) + entry // 2)
+    columns = side[0 : 2 * key_rows, :].T
+    loads[0].wait()
+    loads[4].wait()
     values, lines = [], []
     for p in range(planes):
         value = got[p * gx : (p + 1) * gx].reshape(key_dev, LANES).astype(jnp.int32)
@@ -795,14 +894,17 @@
     for j in range(key_rows):
         at = slice(j * LANES, (j + 1) * LANES)
         hit = columns[:, j : j + 1].astype(jnp.int32) == iota((LANES, key_dev), 1)
-        both = jnp.zeros((LANES, 2 * LANES), F32)
+        chains = [jnp.zeros((LANES, 2 * LANES), F32)] * 2
         for p in range(planes):
-            both = both + dot(jnp.where(hit, lines[p], 0.0).astype(BF16), values[p])
+            chains[p % 2] = chains[p % 2] + dot(
+                jnp.where(hit, lines[p], 0.0).astype(BF16), values[p]
+            )
+        both = joined_chains(chains)
         sums = both[:, :LANES] * 256.0 + both[:, LANES:]
         for h in range(each):
             spot = heavy[device * each + h] - device * key_dev - j * LANES
             line = jnp.sum(
-                jnp.where(iota((extra, LANES), 0) == z * each + h, small, 0.0), axis=0, keepdims=True
+                jnp.where(iota((extra, LANES), 0) == spots[h], small, 0.0), axis=0, keepdims=True
             )
             sums = sums + jnp.where(iota((LANES, LANES), 0) == spot, line, 0.0)
         scale = lax.rsqrt(1.0 + columns[:, key_rows + j : key_rows + j + 1])
@@ -829,31 +931,36 @@
     planes = devices // gx
     cap = max(rows // 32, 3 * rows // (4 * gx)) // 4
     extra = planes * each
-    seg = -(-(cap + extra + len(pieces(cap + extra))) // 16) * 16
+    seg = 2 * (-(-((cap + extra) // 2 + len(pieces(cap + extra + 16))) // 8) * 8)
     deep = -(-cap // LANES) * LANES
     kpp = key_dev // gx
     cfg = dict(
         rows=rows, block=min(rows, 2048), nr=nr, gx=gx, gy=gy, devices=devices,
         own=key_dev * gy, kpp=kpp, key_rows=key_rows, each=each, planes=planes,
-        cap=cap, extra=extra, seg=seg, deep=max(deep, -(-seg // LANES) * LANES),
+        cap=cap, extra=extra, seg=seg, at_once=2 if gx % 2 == 0 else gx, deep=max(deep, -(-seg // LANES) * LANES),
     )
     deep = cfg["deep"]
     table = key_slot.reshape(nr, LANES)
     dma = pltpu.SemaphoreType.DMA
     i16 = jnp.int16
-    got, scales, heads, total, slots = pl.pallas_call(
+    got, scales, heads, side = pl.pallas_call(
         functools.partial(fused, cfg),
         out_shape=(
             shaped(devices, kpp, columns, dtype=i16),
             shaped(devices, 1, LANES),
             shaped(planes, extra, LANES),
-            shaped(key_rows, LANES),
-            shaped(key_rows, LANES),
+            shaped(3 * key_rows, LANES),
         ),
-        in_specs=[ANY] + [VMEM] * 3,
-        out_specs=(ANY,) * 3 + (VMEM,) * 2,
+        in_specs=[ANY] * 4,
+        out_specs=(ANY,) * 4,
         scratch_shapes=[
+            pltpu.VMEM((1, rows), jnp.int32),
+            pltpu.VMEM((1, heavy), jnp.int32),
+            pltpu.VMEM((nr, LANES), jnp.int32),
+            pltpu.VMEM((3 * key_rows, LANES), F32),
             pltpu.VMEM((rows, columns), BF16),
+            pltpu.VMEM((rows, 2 * columns), BF16),
+            pltpu.VMEM((rows // LANES, LANES), F32),
             pltpu.VMEM((nr, rows), BF16),
             pltpu.VMEM((1, rows), jnp.int32),
             pltpu.VMEM((1, rows), jnp.int32),
@@ -873,14 +980,11 @@
             pltpu.VMEM((key_rows, LANES), F32),
             pltpu.VMEM((gx, key_rows, LANES), F32),
             dma,
-            dma((devices,)), dma((devices,)),
-            dma((gx,)), dma((gx,)),
-            dma((gx,)), dma((gx,)),
-            dma((devices,)), dma((devices,)),
-            dma((devices,)), dma((devices,)),
-            dma((planes,)), dma((planes,)),
-            dma((gx,)), dma((gx,)),
             dma((3,)),
+            dma((7,)),
+            dma((7,)),
+            dma((gx,)),
+            dma((4,)),
         ],
         compiler_params=pltpu.CompilerParams(
             collective_id=2, has_side_effects=True, vmem_limit_bytes=LIMIT
@@ -893,11 +997,19 @@
             shaped(each, columns, dtype=BF16),
             shaped(key_rows, LANES),
         ),
-        in_specs=[SMEM] + [VMEM] * 7,
+        in_specs=[SMEM] + [ANY] * 5,
         out_specs=(VMEM,) * 3,
-        scratch_shapes=[pltpu.VMEM((key_dev, LANES), F32)],
+        scratch_shapes=[
+            pltpu.VMEM((key_dev, LANES), F32),
+            pltpu.VMEM((devices, kpp, columns), i16),
+            pltpu.VMEM((devices, 1, LANES), F32),
+            pltpu.VMEM((planes, extra, LANES), F32),
+            pltpu.VMEM((3 * key_rows, LANES), F32),
+            pltpu.VMEM((key_dev, columns), BF16),
+            dma((5,)),
+        ],
         compiler_params=pltpu.CompilerParams(vmem_limit_bytes=LIMIT),
-    )(heavy_keys, got, scales, heads, total, slots, orders, table)
+    )(heavy_keys, got, scales, heads, side, orders)
     return (result, report, slot_rows.reshape(key_dev))
 
 

time: 43.9 us -> 36 us (0.82)
  Pallas kernels: 43.1 us -> 35 us
    pallas_call x1, Pallas kernels: 40.1 us -> 31.7 us  [body(): pl.pallas_call(functools.partial(fused, cfg), out_shape=(shaped(devices,...]
where the time goes in v2:
time: 36 us; the launch traced here: 35.8 us
  Pallas kernels  35 us (97%)
  between operations  0.8 us (2%)
    pallas_call x1, Pallas kernels, body(): pl.pallas_call(functools.partial(fused, cfg), out_shape=(shaped(devices,...  31.7 us
    pallas_call x1, Pallas kernels, body(): pl.pallas_call(functools.partial(join, cfg), out_shape=(shaped(key_dev, c...  3.34 us

profile of v2, /device:TPU:0, one launch (start us, length us, event | category | flops | bytes accessed | tf_op | source)
XLA Modules:
  0.0 35.8 jit_solution(14547544255680562848)
XLA Ops:
  0.6 31.7 %shard_map.76 = (s16[32,64,128]{2,1,0:T(8,128)(2,1)}, f32[32,1,128]{2,1,0:T(1,128)}, f32[4,8,128]{2,1,0:T(8,128)}, f32[12,128]{1,0:T(8,128)}) custom-call(bf16[8192,128]{1,0:T(8,128)(2,1)} %measures.1, s32[1,8192]{1,0:T(1,128)} %bitcast.5, s32[1,64]{1,0:T(1,128)} %bitcast.6, s32[128,128]{1,0:T(8,128)} %bitcast.4), custom_call_target="tpu_custom_call" | custom-call | tf_op jit(solution)/shard_map/pallas_call | solution.py:946
  32.3 3.3 %shard_map.77 = (bf16[512,128]{1,0:T(8,128)(2,1)}, bf16[2,128]{1,0:T(2,128)(2,1)}, f32[4,128]{1,0:T(4,128)}) custom-call(s32[64]{0:T(128)} %heavy.1, s16[32,64,128]{2,1,0:T(8,128)(2,1)} %get-tuple-element.10.got_hbm, f32[32,1,128]{2,1,0:T(1,128)} %get-tuple-element.11.scales_hbm, f32[4,8,128]{2,1,0:T(8,128)} %get-tuple-element.12.heads_hbm, ...), custom_call_target="tpu_custom_call" | custom-call | tf_op jit(solution)/shard_map/pallas_call | solution.py:993

commit v3 on v2

--- a/solution.py
+++ b/solution.py
@@ -521,6 +521,16 @@
     load = pltpu.make_async_copy(measures, rows_in, load_sem)
     load.start()
 
+    steps_to = sorted(range(1, gx), key=lambda m: (-bin(m >> 1).count("1"), m & 1, -m)) + [0]
+    partner = []
+    for m in steps_to:
+        x, bit = j, 1
+        while bit < gx:
+            if m & bit:
+                x = x + bit * (1 - 2 * lax.rem(x // bit, 2))
+            bit *= 2
+        partner.append(x)
+
     barrier = pltpu.get_barrier_semaphore()
 
     every_other(
@@ -574,38 +584,34 @@
     local = jnp.where(
         light, local, (cap + (block_of // gx) * each + lax.rem(head, each)).astype(F32)
     )
-    tables = jnp.concatenate([group.astype(F32).T, local.T], axis=0).astype(BF16)
+    tables = jnp.concatenate([256.0 * group.astype(F32).T, local.T], axis=1).astype(BF16)
+    pl.semaphore_wait(barrier, devices - 1)
+
+    for s in range(gx - 1):
+        remote(
+            hist16, goth.at[s], out_sem.at[HISTS], back_sem.at[HISTS], in_plane(z, partner[s])
+        ).start()
+    every_other(
+        lambda d, where: remote(
+            hist.at[d], cnt_got.at[me], out_sem.at[COUNTS], back_sem.at[COUNTS], where
+        ).start()
+    )
+
+    load.wait()
     for c in range(rows // block):
         span = slice(c * block, (c + 1) * block)
-        spread = dot(tables, seg_hot[:, span])
+        row_hot = seg_hot[:, span]
+        spread = dot(tables, jnp.concatenate([row_hot, row_hot], axis=0))
         mask = iota((LANES, block), 0) == (keys[:, span] & 127)
-        group_row[:, span] = jnp.sum(
-            jnp.where(mask, spread[:LANES], 0.0), axis=0, keepdims=True
-        ).astype(jnp.int32)
-        inside = jnp.sum(
-            jnp.where(mask, spread[LANES:], 0.0), axis=0, keepdims=True
-        ).astype(jnp.int32)
+        both = jnp.sum(jnp.where(mask, spread, 0.0), axis=0, keepdims=True).astype(jnp.int32)
+        group_row[:, span] = both >> 8
+        inside = both & 255
         local_row[:, span] = inside >> 1
         odd = (inside & 1).astype(F32)
         for i in range(block // LANES):
             at = c * (block // LANES) + i
             parity[at : at + 1, :] = odd[:, i * LANES : (i + 1) * LANES]
 
-    pl.semaphore_wait(barrier, devices - 1)
-
-    @pl.loop(0, gx - 1)
-    def _(s):
-        x = lax.rem(j + 1 + s, gx)
-        t = lax.rem(2 * gx - 2 - s, gx)
-        remote(hist16, goth.at[t], out_sem.at[HISTS], back_sem.at[HISTS], in_plane(z, x)).start()
-
-    every_other(
-        lambda d, where: remote(
-            hist.at[d], cnt_got.at[me], out_sem.at[COUNTS], back_sem.at[COUNTS], where
-        ).start()
-    )
-
-    load.wait()
     turned = parity[...].T
     for c in range(rows // LANES):
         span = slice(c * LANES, (c + 1) * LANES)
@@ -629,7 +635,7 @@
             hot = [
                 jnp.where(
                     iota((half_seg, block), 0)
-                    == jnp.where(group == lax.rem(j + 1 + s, gx), local, -1),
+                    == jnp.where(group == partner[s], local, -1),
                     1.0,
                     0.0,
                 )
@@ -655,10 +661,9 @@
             whole = jnp.concatenate([fixed[:used], foot, fixed[half_seg:]], axis=0)
             send1[s] = whole.astype(jnp.int32).astype(jnp.int16)
             if s < gx - 1:
-                t = (2 * gx - 2 - s) % gx
                 remote(
-                    send1.at[s], got1.at[t], out_sem.at[ROWS], row_sem.at[t],
-                    in_plane(z, lax.rem(j + 1 + s, gx)),
+                    send1.at[s], got1.at[s], out_sem.at[ROWS], row_sem.at[s],
+                    in_plane(z, partner[s]),
                 ).start()
 
     def all_of(ref, kind, number):
@@ -761,42 +766,52 @@
         ]
     else:
         order = [lax.rem(z + s, planes) for s in range(1, planes + 1)]
+    diagonal = iota((kpp, LANES), 1) == iota((kpp, LANES), 0) + shift
+    wave = gx // 2
+    part = wave * kpp
     for c in range(planes):
-        far = order[c]
-        spot = found[pl.ds(pl.multiple_of(far * chunk, chunk), chunk), :]
-        chains = [jnp.zeros((chunk, 2 * LANES), F32)] * 2
-        for t in range(gx):
-            hit = spot[:, t : t + 1] == lanes
-            chains[t % 2] = chains[t % 2] + dot(
-                jnp.where(hit, powers[t], 0.0).astype(BF16), wide[t]
+        far, last = order[c], c == planes - 1
+        for first in range(0, gx, wave):
+            top = pl.multiple_of(far * chunk + first * kpp, part)
+            spot = found[pl.ds(top, part), :]
+            chains = [jnp.zeros((part, 2 * LANES), F32)] * 2
+            for t in range(gx):
+                hit = spot[:, t : t + 1] == lanes
+                chains[t % 2] = chains[t % 2] + dot(
+                    jnp.where(hit, powers[t], 0.0).astype(BF16), wide[t]
+                )
+            acc = joined_chains(chains)
+            fixed, power = encode(acc[:, :LANES] * 256.0 + acc[:, LANES:])
+            send2[c, first : first + wave] = (
+                fixed.astype(jnp.int32).astype(jnp.int16).reshape(wave, kpp, LANES)
             )
-        acc = joined_chains(chains)
-        fixed, power = encode(acc[:, :LANES] * 256.0 + acc[:, LANES:])
-        send2[c] = fixed.astype(jnp.int32).astype(jnp.int16).reshape(gx, kpp, LANES)
-        scale = jnp.exp2(power - 15.0)
-        diagonal = iota((kpp, LANES), 1) == iota((kpp, LANES), 0) + shift
-        for x in range(gx):
-            srow[c, x] = jnp.sum(
-                jnp.where(diagonal, scale[x * kpp : (x + 1) * kpp], 0.0), axis=0, keepdims=True
-            )
-        last = c == planes - 1
-
-        @pl.loop(0, gx - 1 if last else gx)
-        def _(s):
-            x = lax.rem(j + 1 + s, gx)
-            where = in_plane(far, x)
-            remote(
-                send2.at[c, x], got2.at[me], out_sem.at[MERGED], back_sem.at[MERGED], where
-            ).start()
-            remote(
-                srow.at[c, x], scales2.at[me], out_sem.at[SCALES], back_sem.at[SCALES], where
-            ).start()
-
-        if last:
-            keep = pltpu.make_async_copy(send2.at[c, j], got2.at[me], own_sem.at[1])
-            keep.start()
-            keep_row = pltpu.make_async_copy(srow.at[c, j], scales2.at[me], own_sem.at[2])
-            keep_row.start()
+            scale = jnp.exp2(power - 15.0)
+            for x in range(wave):
+                srow[c, first + x] = jnp.sum(
+                    jnp.where(diagonal, scale[x * kpp : (x + 1) * kpp], 0.0), axis=0, keepdims=True
+                )
+
+            def one_block(x, c=c, far=far):
+                where = in_plane(far, x)
+                remote(
+                    send2.at[c, x], got2.at[me], out_sem.at[MERGED], back_sem.at[MERGED], where
+                ).start()
+                remote(
+                    srow.at[c, x], scales2.at[me], out_sem.at[SCALES], back_sem.at[SCALES], where
+                ).start()
+
+            @pl.loop(0, wave)
+            def _(s, first=first, last=last, one_block=one_block):
+                x = first + lax.rem(j + s, wave)
+                if last:
+                    pl.when(x != j)(lambda: one_block(x))
+                else:
+                    one_block(x)
+
+    keep = pltpu.make_async_copy(send2.at[planes - 1, j], got2.at[me], own_sem.at[1])
+    keep.start()
+    keep_row = pltpu.make_async_copy(srow.at[planes - 1, j], scales2.at[me], own_sem.at[2])
+    keep_row.start()
 
     all_of(tgot, TOTALS, gx - 1).wait()
 
@@ -833,6 +848,7 @@
         inside = rank[x * key_rows : (x + 1) * key_rows] + float(x * kpp)
         place = place + jnp.where(owner == x, inside, 0.0)
     side[0:key_rows, :] = place
+    side[3 * key_rows : 4 * key_rows, :] = codes[me] - (each * me).astype(F32)
     hand_over = pltpu.make_async_copy(side, side_out, own_sem.at[3])
     hand_over.start()
 
@@ -848,42 +864,37 @@
 
 
 def join(
-    cfg, heavy, got_hbm, scales_hbm, heads_hbm, side_hbm, orders_hbm, result, report, slot_rows,
-    joined, got, scales, heads, side, orders, sems,
+    cfg, got_hbm, scales_hbm, heads_hbm, side_hbm, orders_hbm, result, report, slot_rows,
+    got, scales, heads, side, orders, done, lines_out, sems, out_sems,
 ):
     gx, gy, kpp = cfg["gx"], cfg["gy"], cfg["kpp"]
     key_rows, each, planes, extra = cfg["key_rows"], cfg["each"], cfg["planes"], cfg["extra"]
     key_dev = key_rows * LANES
     per_tile = LANES // kpp
     loads = [
+        pltpu.make_async_copy(got_hbm.at[p * gx : (p + 1) * gx], got.at[p], sems.at[4 + p])
+        for p in range(planes)
+    ]
+    tables = [
         pltpu.make_async_copy(source, target, sems.at[i])
         for i, (source, target) in enumerate(
-            [(got_hbm, got), (side_hbm, side), (scales_hbm, scales), (heads_hbm, heads), (orders_hbm, orders)]
+            [(side_hbm, side), (scales_hbm, scales), (heads_hbm, heads), (orders_hbm, orders)]
         )
     ]
-    for one in loads:
+    for one in tables[:2] + loads + tables[2:]:
         one.start()
-    device = lax.axis_index("gx") * gy + lax.axis_index("gy")
-    z = device // gx
-    for one in loads[1:4]:
-        one.wait()
-    slot_rows[...] = side[2 * key_rows : 3 * key_rows, :]
-    small = heads[0]
-    for p in range(1, planes):
-        small = small + heads[p]
-    spots = []
-    for h in range(each):
-        entry = z * each + h
-        spots.append(lax.rem(entry, 2) * (extra // 2) + entry // 2)
-    columns = side[0 : 2 * key_rows, :].T
-    loads[0].wait()
-    loads[4].wait()
-    values, lines = [], []
+    z = (lax.axis_index("gx") * gy + lax.axis_index("gy")) // gx
+    tables[0].wait()
+    tables[1].wait()
+    columns = side[...].T
+    stores = [
+        pltpu.make_async_copy(
+            side.at[2 * key_rows : 3 * key_rows, :], slot_rows, out_sems.at[key_rows]
+        )
+    ]
+    stores[0].start()
+    lines = []
     for p in range(planes):
-        value = got[p * gx : (p + 1) * gx].reshape(key_dev, LANES).astype(jnp.int32)
-        values.append(
-            jnp.concatenate([(value >> 8).astype(F32), (value & 255).astype(F32)], axis=1).astype(BF16)
-        )
         tiles = []
         for x in range(0, gx, per_tile):
             tile = scales[p * gx + x]
@@ -891,9 +902,29 @@
                 tile = tile + scales[p * gx + x + i]
             tiles.append(tile)
         lines.append(jnp.concatenate(tiles, axis=1))
-    for j in range(key_rows):
-        at = slice(j * LANES, (j + 1) * LANES)
-        hit = columns[:, j : j + 1].astype(jnp.int32) == iota((LANES, key_dev), 1)
+    tables[2].wait()
+    tables[3].wait()
+    small = heads[0]
+    for p in range(1, planes):
+        small = small + heads[p]
+    own_lines = []
+    for h in range(each):
+        entry = z * each + h
+        spot = lax.rem(entry, 2) * (extra // 2) + entry // 2
+        own_lines.append(
+            jnp.sum(jnp.where(iota((extra, LANES), 0) == spot, small, 0.0), axis=0, keepdims=True)
+        )
+    values = []
+    for p in range(planes):
+        loads[p].wait()
+        value = got[p].reshape(key_dev, LANES).astype(jnp.int32)
+        values.append(
+            jnp.concatenate([(value >> 8).astype(F32), (value & 255).astype(F32)], axis=1).astype(BF16)
+        )
+    picked = [jnp.zeros((1, LANES), F32)] * each
+    for q in range(key_rows):
+        at = slice(q * LANES, (q + 1) * LANES)
+        hit = columns[:, q : q + 1] == iota((LANES, key_dev), 1).astype(F32)
         chains = [jnp.zeros((LANES, 2 * LANES), F32)] * 2
         for p in range(planes):
             chains[p % 2] = chains[p % 2] + dot(
@@ -901,20 +932,23 @@
             )
         both = joined_chains(chains)
         sums = both[:, :LANES] * 256.0 + both[:, LANES:]
+        head = columns[:, 3 * key_rows + q : 3 * key_rows + q + 1]
         for h in range(each):
-            spot = heavy[device * each + h] - device * key_dev - j * LANES
-            line = jnp.sum(
-                jnp.where(iota((extra, LANES), 0) == spots[h], small, 0.0), axis=0, keepdims=True
+            sums = sums + jnp.where(head == float(h + 1), own_lines[h], 0.0)
+        scale = lax.rsqrt(1.0 + columns[:, key_rows + q : key_rows + q + 1])
+        value = orders[at, :].astype(F32) * sums * scale
+        for h in range(each):
+            picked[h] = picked[h] + jnp.sum(
+                jnp.where(head == float(h + 1), value, 0.0), axis=0, keepdims=True
             )
-            sums = sums + jnp.where(iota((LANES, LANES), 0) == spot, line, 0.0)
-        scale = lax.rsqrt(1.0 + columns[:, key_rows + j : key_rows + j + 1])
-        value = orders[at, :].astype(F32) * sums * scale
-        joined[at, :] = value
-        result[at, :] = value.astype(BF16)
-    picked = [
-        joined[pl.ds(heavy[device * each + h] - device * key_dev, 1), :] for h in range(each)
-    ]
-    report[...] = jnp.concatenate(picked, axis=0).astype(BF16)
+        done[at, :] = value.astype(BF16)
+        stores.append(pltpu.make_async_copy(done.at[at, :], result.at[at, :], out_sems.at[q]))
+        stores[-1].start()
+    lines_out[...] = jnp.concatenate(picked, axis=0).astype(BF16)
+    stores.append(pltpu.make_async_copy(lines_out, report, out_sems.at[key_rows + 1]))
+    stores[-1].start()
+    for one in stores:
+        one.wait()
 
 
 def body(measures, row_keys, orders, heavy_keys, key_slot):
@@ -926,7 +960,7 @@
     nr = key_slot.shape[0] // LANES
     heavy = heavy_keys.shape[0]
     each = heavy // devices
-    if gx * nr > 2048:
+    if gx * nr > 2048 or gx & (gx - 1):
         return split_body(measures, row_keys, orders, heavy_keys, key_slot)
     planes = devices // gx
     cap = max(rows // 32, 3 * rows // (4 * gx)) // 4
@@ -949,7 +983,7 @@
             shaped(devices, kpp, columns, dtype=i16),
             shaped(devices, 1, LANES),
             shaped(planes, extra, LANES),
-            shaped(3 * key_rows, LANES),
+            shaped(4 * key_rows, LANES),
         ),
         in_specs=[ANY] * 4,
         out_specs=(ANY,) * 4,
@@ -957,7 +991,7 @@
             pltpu.VMEM((1, rows), jnp.int32),
             pltpu.VMEM((1, heavy), jnp.int32),
             pltpu.VMEM((nr, LANES), jnp.int32),
-            pltpu.VMEM((3 * key_rows, LANES), F32),
+            pltpu.VMEM((4 * key_rows, LANES), F32),
             pltpu.VMEM((rows, columns), BF16),
             pltpu.VMEM((rows, 2 * columns), BF16),
             pltpu.VMEM((rows // LANES, LANES), F32),
@@ -997,19 +1031,21 @@
             shaped(each, columns, dtype=BF16),
             shaped(key_rows, LANES),
         ),
-        in_specs=[SMEM] + [ANY] * 5,
-        out_specs=(VMEM,) * 3,
+        in_specs=[ANY] * 5,
+        out_specs=(ANY,) * 3,
         scratch_shapes=[
-            pltpu.VMEM((key_dev, LANES), F32),
-            pltpu.VMEM((devices, kpp, columns), i16),
+            pltpu.VMEM((planes, gx, kpp, columns), i16),
             pltpu.VMEM((devices, 1, LANES), F32),
             pltpu.VMEM((planes, extra, LANES), F32),
-            pltpu.VMEM((3 * key_rows, LANES), F32),
+            pltpu.VMEM((4 * key_rows, LANES), F32),
             pltpu.VMEM((key_dev, columns), BF16),
-            dma((5,)),
+            pltpu.VMEM((key_dev, columns), BF16),
+            pltpu.VMEM((each, columns), BF16),
+            dma((4 + planes,)),
+            dma((key_rows + 2,)),
         ],
         compiler_params=pltpu.CompilerParams(vmem_limit_bytes=LIMIT),
-    )(heavy_keys, got, scales, heads, side, orders)
+    )(got, scales, heads, side, orders)
     return (result, report, slot_rows.reshape(key_dev))
 
 

time: 36 us -> 34.7 us (0.964)
  Pallas kernels: 35 us -> 33.7 us
    pallas_call x1, Pallas kernels: 31.7 us -> 30.7 us  [body(): pl.pallas_call(functools.partial(fused, cfg), out_shape=(shaped(devices,...]
    pallas_call x1, Pallas kernels: 3.34 us -> 2.96 us  [body(): pl.pallas_call(functools.partial(join, cfg), out_shape=(shaped(key_dev, c...]
where the time goes in v3:
time: 34.7 us; the launch traced here: 34.5 us
  Pallas kernels  33.7 us (97%)
  between operations  0.8 us (2%)
    pallas_call x1, Pallas kernels, body(): pl.pallas_call(functools.partial(fused, cfg), out_shape=(shaped(devices,...  30.7 us
    pallas_call x1, Pallas kernels, body(): pl.pallas_call(functools.partial(join, cfg), out_shape=(shaped(key_dev, c...  2.96 us

profile of v3, /device:TPU:0, one launch (start us, length us, event | category | flops | bytes accessed | tf_op | source)
XLA Modules:
  0.0 34.5 jit_solution(9676217615369047397)
XLA Ops:
  0.6 30.7 %shard_map.76 = (s16[32,64,128]{2,1,0:T(8,128)(2,1)}, f32[32,1,128]{2,1,0:T(1,128)}, f32[4,8,128]{2,1,0:T(8,128)}, f32[16,128]{1,0:T(8,128)}) custom-call(bf16[8192,128]{1,0:T(8,128)(2,1)} %measures.1, s32[1,8192]{1,0:T(1,128)} %bitcast.5, s32[1,64]{1,0:T(1,128)} %bitcast.6, s32[128,128]{1,0:T(8,128)} %bitcast.4), custom_call_target="tpu_custom_call" | custom-call | tf_op jit(solution)/shard_map/pallas_call | solution.py:980
  31.3 3.0 %shard_map.77 = (bf16[512,128]{1,0:T(8,128)(2,1)}, bf16[2,128]{1,0:T(2,128)(2,1)}, f32[4,128]{1,0:T(4,128)}) custom-call(s16[32,64,128]{2,1,0:T(8,128)(2,1)} %get-tuple-element.10.got_hbm, f32[32,1,128]{2,1,0:T(1,128)} %get-tuple-element.11.scales_hbm, f32[4,8,128]{2,1,0:T(8,128)} %get-tuple-element.12.heads_hbm, f32[16,128]{1,0:T(8,128)} %get-tuple-element.13.side_hbm, ...), custom_call_target="tpu_custom_call" | custom-call | tf_op jit(solution)/shard_map/pallas_call | solution.py:1027

commit v4 on v3

--- a/solution.py
+++ b/solution.py
@@ -598,7 +598,8 @@
     )
 
     load.wait()
-    for c in range(rows // block):
+    for c in range(rows // min(block, 512)):
+        block = min(cfg["block"], 512)
         span = slice(c * block, (c + 1) * block)
         row_hot = seg_hot[:, span]
         spread = dot(tables, jnp.concatenate([row_hot, row_hot], axis=0))
@@ -612,8 +613,10 @@
             at = c * (block // LANES) + i
             parity[at : at + 1, :] = odd[:, i * LANES : (i + 1) * LANES]
 
+    block = cfg["block"]
     turned = parity[...].T
-    for c in range(rows // LANES):
+
+    def halves(c):
         span = slice(c * LANES, (c + 1) * LANES)
         line = rows_in[span, :]
         odd = line * jnp.broadcast_to(turned[:, c : c + 1], (LANES, LANES)).astype(BF16)
@@ -632,6 +635,9 @@
         for c in range(rows // block):
             span = slice(c * block, (c + 1) * block)
             group, local = group_row[:, span], local_row[:, span]
+            if first == 0:
+                for i in range(c * block // LANES, (c + 1) * block // LANES):
+                    halves(i)
             hot = [
                 jnp.where(
                     iota((half_seg, block), 0)
@@ -789,7 +795,7 @@
             for x in range(wave):
                 srow[c, first + x] = jnp.sum(
                     jnp.where(diagonal, scale[x * kpp : (x + 1) * kpp], 0.0), axis=0, keepdims=True
-                )
+                ).astype(BF16)
 
             def one_block(x, c=c, far=far):
                 where = in_plane(far, x)
@@ -897,9 +903,9 @@
     for p in range(planes):
         tiles = []
         for x in range(0, gx, per_tile):
-            tile = scales[p * gx + x]
+            tile = scales[p * gx + x].astype(F32)
             for i in range(1, per_tile):
-                tile = tile + scales[p * gx + x + i]
+                tile = tile + scales[p * gx + x + i].astype(F32)
             tiles.append(tile)
         lines.append(jnp.concatenate(tiles, axis=1))
     tables[2].wait()
@@ -981,7 +987,7 @@
         functools.partial(fused, cfg),
         out_shape=(
             shaped(devices, kpp, columns, dtype=i16),
-            shaped(devices, 1, LANES),
+            shaped(devices, 1, LANES, dtype=BF16),
             shaped(planes, extra, LANES),
             shaped(4 * key_rows, LANES),
         ),
@@ -1010,7 +1016,7 @@
             pltpu.VMEM((gx, deep, 2 * LANES), BF16),
             pltpu.VMEM((extra, LANES), F32),
             pltpu.VMEM((planes, gx, kpp, LANES), i16),
-            pltpu.VMEM((planes, gx, 1, LANES), F32),
+            pltpu.VMEM((planes, gx, 1, LANES), BF16),
             pltpu.VMEM((key_rows, LANES), F32),
             pltpu.VMEM((gx, key_rows, LANES), F32),
             dma,
@@ -1035,7 +1041,7 @@
         out_specs=(ANY,) * 3,
         scratch_shapes=[
             pltpu.VMEM((planes, gx, kpp, columns), i16),
-            pltpu.VMEM((devices, 1, LANES), F32),
+            pltpu.VMEM((devices, 1, LANES), BF16),
             pltpu.VMEM((planes, extra, LANES), F32),
             pltpu.VMEM((4 * key_rows, LANES), F32),
             pltpu.VMEM((key_dev, columns), BF16),

time: 34.7 us -> 34.6 us (level)
  no operation moved by 1% of the time
where the time goes in v4:
time: 34.6 us; the launch traced here: 34.4 us
  Pallas kernels  33.6 us (97%)
  between operations  0.8 us (2%)
    pallas_call x1, Pallas kernels, body(): pl.pallas_call(functools.partial(fused, cfg), out_shape=(shaped(devices,...  30.6 us
    pallas_call x1, Pallas kernels, body(): pl.pallas_call(functools.partial(join, cfg), out_shape=(shaped(key_dev, c...  2.96 us

profile of v4, /device:TPU:0, one launch (start us, length us, event | category | flops | bytes accessed | tf_op | source)
XLA Modules:
  0.0 34.4 jit_solution(1176967189713819256)
XLA Ops:
  0.6 30.6 %shard_map.76 = (s16[32,64,128]{2,1,0:T(8,128)(2,1)}, bf16[32,1,128]{2,1,0:T(2,128)(2,1)}, f32[4,8,128]{2,1,0:T(8,128)}, f32[16,128]{1,0:T(8,128)}) custom-call(bf16[8192,128]{1,0:T(8,128)(2,1)} %measures.1, s32[1,8192]{1,0:T(1,128)} %bitcast.5, s32[1,64]{1,0:T(1,128)} %bitcast.6, s32[128,128]{1,0:T(8,128)} %bitcast.4), custom_call_target="tpu_custom_call" | custom-call | tf_op jit(solution)/shard_map/pallas_call | solution.py:986
  31.3 3.0 %shard_map.77 = (bf16[512,128]{1,0:T(8,128)(2,1)}, bf16[2,128]{1,0:T(2,128)(2,1)}, f32[4,128]{1,0:T(4,128)}) custom-call(s16[32,64,128]{2,1,0:T(8,128)(2,1)} %get-tuple-element.10.got_hbm, bf16[32,1,128]{2,1,0:T(2,128)(2,1)} %get-tuple-element.11.scales_hbm, f32[4,8,128]{2,1,0:T(8,128)} %get-tuple-element.12.heads_hbm, ...), custom_call_target="tpu_custom_call" | custom-call | tf_op jit(solution)/shard_map/pallas_call | solution.py:1033
